TPU v7x, 512 devices: a whole 4x8x8 slice. The times are simulated.
512 devices in a mesh: ctx: 256 (over z, y, x_hi, core), tp: 2 (over x_lo).
Axes of the slice: x: 4 (x_hi: 2, x_lo: 2; x = x_hi * 2 + x_lo), y: 8, z: 8, core: 2. Of those that a mesh axis runs over, the one named last changes fastest.
Arguments:
- queries: bfloat16 [16384, 16, 128], P('ctx', 'tp'), may hold values from -6 to 6
- incoming_lookup_vectors: bfloat16 [16384, 4, 128], P('ctx', 'tp'), may hold values from -6 to 6
- incoming_content_vectors: bfloat16 [16384, 4, 128], P('ctx', 'tp'), may hold values from -6 to 6
Outputs:
- attention: bfloat16 [16384, 16, 128], P(('ctx', 'tp'))
- key_cache: bfloat16 [16384, 4, 128], P('ctx', 'tp')
All inputs are finite; a program needn't handle non-finite values.
Results may differ from a plain program's by a relative error of at most 0.0075.
Values may be sent and summed in bfloat16 or wider, within the bound.
A program may use at most 128 MiB of HBM per device.

v0:
```python
import math

import jax
import jax.numpy as jnp
from jax import lax
from jax.sharding import PartitionSpec as P

rope_base = 500000.0


def rotate(tensor, positions):
    feature_width = tensor.shape[-1]
    half_width = feature_width // 2
    inverse_freq = rope_base ** (-(jnp.arange(half_width, dtype=jnp.float32) * 2.0 / feature_width))
    angles = positions.astype(jnp.float32)[:, None] * inverse_freq[None, :]
    cosine = jnp.cos(angles)[:, None, :]
    sine_part = jnp.sin(angles)[:, None, :]
    widened = tensor.astype(jnp.float32)
    front_half = widened[..., :half_width]
    second = widened[..., half_width:]
    return jnp.concatenate(
        [front_half * cosine - second * sine_part, second * cosine + front_half * sine_part],
        axis=-1,
    ).astype(jnp.bfloat16)


def absorb(running, q_block, query_pos, key_piece, value_piece, key_pos, score_scale):
    run_max, run_sum, run_acc = running
    scores = (
        jnp.einsum("sjgd,tjd->sjgt", q_block, key_piece, preferred_element_type=jnp.float32)
        * score_scale
    )
    visible = (query_pos[:, None] >= key_pos[None, :])[:, None, None, :]
    scores = jnp.where(visible, scores, -jnp.inf)
    new_max = jnp.maximum(run_max, jnp.max(scores, axis=-1))
    weights = jnp.exp(scores - new_max[..., None])
    factor = jnp.exp(run_max - new_max)
    new_sum = factor * run_sum + jnp.sum(weights, axis=-1)
    new_acc = factor[..., None] * run_acc + jnp.einsum(
        "sjgt,tjd->sjgd", weights, value_piece.astype(jnp.float32)
    )
    return (new_max, new_sum, new_acc)


def per_device(queries, incoming_lookup_vectors, incoming_content_vectors):
    tok_rows = queries.shape[0]
    half_rows = tok_rows // 2
    head_size = queries.shape[2]
    local_heads = queries.shape[1]
    local_kv = incoming_lookup_vectors.shape[1]
    heads_per_share = local_heads // local_kv
    my_index = lax.axis_index("ctx")
    score_scale = 1.0 / math.sqrt(head_size)
    natural_pos = my_index * tok_rows + jnp.arange(tok_rows, dtype=jnp.int32)
    key_cache = rotate(incoming_lookup_vectors, natural_pos)
    spun_vectors = rotate(queries, natural_pos)

    def place(global_rows):
        return global_rows

    q_grouped = spun_vectors.reshape(tok_rows, local_kv, heads_per_share, head_size)

    def fold_step(running, piece):
        key_piece, value_piece = piece
        piece_len = key_piece.shape[0]
        key_pos = place(jnp.arange(piece_len, dtype=jnp.int32))
        nearest = jnp.min(key_pos)
        updated_halves = []
        for half_index in range(2):
            lo_row = half_index * half_rows
            portion = tuple((member[lo_row : lo_row + half_rows] for member in running))
            q_block = q_grouped[lo_row : lo_row + half_rows]
            block_pos = natural_pos[lo_row : lo_row + half_rows]
            updated = lax.cond(
                nearest <= jnp.max(block_pos),
                lambda current: absorb(
                    current, q_block, block_pos, key_piece, value_piece, key_pos, score_scale
                ),
                lambda current: current,
                portion,
            )
            updated_halves.append(updated)
        return tuple(
            (
                jnp.concatenate([updated_halves[0][slot], updated_halves[1][slot]], axis=0)
                for slot in range(3)
            )
        )

    start_max = jnp.full((tok_rows, local_kv, heads_per_share), -1e30, jnp.float32)
    start_sum = jnp.zeros((tok_rows, local_kv, heads_per_share), jnp.float32)
    start_acc = jnp.zeros((tok_rows, local_kv, heads_per_share, head_size), jnp.float32)
    run_max, run_sum, run_acc = fold_step(
        (start_max, start_sum, start_acc),
        (
            lax.all_gather(key_cache, "ctx", axis=0, tiled=True),
            lax.all_gather(incoming_content_vectors, "ctx", axis=0, tiled=True),
        ),
    )
    result = (
        (run_acc / run_sum[..., None])
        .reshape(tok_rows, local_heads, head_size)
        .astype(jnp.bfloat16)
    )
    attention = lax.all_to_all(result, "tp", split_axis=0, concat_axis=1, tiled=True)
    return (attention, key_cache)


def solution(mesh):
    return jax.shard_map(
        per_device,
        mesh=mesh,
        in_specs=(P("ctx", "tp", None), P("ctx", "tp", None), P("ctx", "tp", None)),
        out_specs=(P(("ctx", "tp"), None, None), P("ctx", "tp", None)),
        check_vma=False,
    )
```

profile of v0, /device:TPU:1, one launch (start us, length us, event | category | flops | bytes accessed | tf_op | source)
XLA Modules:
  0.0 382.6 jit_solution(14098692819505498980)
XLA Ops:
  7.2 0.0 all-gather.5.cloned.1.call-start
  7.2 1.4 copy.11
  8.6 0.0 all-gather.5.cloned.1.call-update
  8.6 0.0 all-gather.3.cloned.1.call-start
  8.7 0.8 convert_element_type.30
  9.5 0.2 multiply_cosine_fusion
  9.7 0.2 subtract_convert_fusion.1
  9.9 0.7 pad_maximum_fusion.1
  10.6 0.0 all-gather.3.cloned.1.call-update
  10.6 0.8 slice_reduce_fusion.1
  12.7 0.9 copy_convert_fusion
  13.6 0.2 subtract_convert_fusion
  13.7 0.1 pad_maximum_fusion
  13.9 143.8 %all-gather.5.cloned.1.call-done = bf16[16384,2,128]{2,0,1:T(8,128)(2,1)} async-done(((bf16[64,2,128]{2,0,1:T(8,128)(2,1)}), bf16[16384,2,128]{2,0,1:T(8,128)(2,1)}) %all-gather.5.cloned.1.call-update) | async-done | bytes 8388624 | tf_op jit(solution)/shard_map/all_gather | solution.py:97
  157.6 139.7 %all-gather.3.cloned.1.call-done = bf16[16384,2,128]{2,1,0:T(2,128)(2,1)} async-done(((bf16[64,2,128]{2,1,0:T(2,128)(2,1)}), bf16[16384,2,128]{2,1,0:T(2,128)(2,1)}) %all-gather.3.cloned.1.call-update) | async-done | bytes 8388624 | tf_op jit(solution)/shard_map/all_gather | solution.py:96
  297.4 35.7 %conditional.2 = (f32[32,2,4]{0,2,1:T(4,128)S(1)}, f32[32,8,128]{2,1,0:T(8,128)S(1)}) conditional(s32[]{:T(128)} %convert_element_type.27, () %tuple.28, (s32[32]{0:T(128)S(1)}, s32[16384]{0:T(1024)S(1)}, bf16[64,8,128]{2,0,1:T(8,128)(2,1)S(1)}, bf16[16384,2,128]{2,1,0:T(2,128)(2,1)}, bf16[16384,2,128]{2,0,1:T(8,128)(2,1)}) %tuple.29), branch_computations={%region_1.0_spmd, %region_2.5_spmd} | conditional | flops 2173207296 | bytes 68824208 | solution.py:74
  297.4 0.3 broadcast_compare_fusion
  297.7 16.1 %fusion.30 = (f32[32,2,4]{0,2,1:T(4,128)S(1)}, f32[32,2,4,16384]{3,0,2,1:T(8,128)}) fusion(bf16[32,2,4,128]{3,0,2,1:T(8,128)(2,1)S(1)} %bitcast.53, bf16[16384,2,128,1]{2,1,0,3:T(2,128)(2,1)} %bitcast.56, pred[32,16384]{1,0:T(8,128)(4,1)S(1)} %broadcast_compare_fusion), kind=kOutput, calls=%fused_computation.48 | convolution fusion | flops 1086324480 | bytes 25756672 | tf_op jit(solution)/shard_map/cond/branch_1_fun/sjgd,tjd->sjgt/dot_general | solution.py:30
  313.9 8.1 %fusion.3 = f32[32,2,4]{0,2,1:T(4,128)S(1)} fusion(f32[32,2,4,16384]{3,0,2,1:T(8,128)} %get-tuple-element.73, f32[32,2,4]{0,2,1:T(4,128)S(1)} %broadcast_maximum_fusion), kind=kLoop, calls=%fused_computation.5 | loop fusion | flops 8388352 | bytes 16779264 | tf_op jit(solution)/shard_map/cond/branch_1_fun/reduce_sum | solution.py:38
  322.0 11.0 %fusion.10 = f32[32,2,4,128]{3,0,2,1:T(8,128)S(1)} fusion(bf16[16384,2,128]{2,0,1:T(8,128)(2,1)} %get-tuple-element.30, f32[32,2,4,16384]{3,0,2,1:T(8,128)} %get-tuple-element.73, f32[32,2,4]{0,2,1:T(4,128)S(1)} %broadcast_maximum_fusion, f32[32,2,4]{0,2,1:T(4,128)S(1)} %get-tuple-element.70), kind=kOutput, calls=%fused_computation.10 | convolution fusion | flops 1077968896 | bytes 25298944 | tf_op jit(solution)/shard_map/cond/branch_1_fun/sjgt,tjd->sjgd/dot_general | solution.py:39
  333.0 0.1 copy.27
  333.1 35.9 %conditional.3 = (f32[32,2,4]{0,2,1:T(4,128)S(1)}, f32[32,8,128]{2,1,0:T(8,128)S(1)}) conditional(s32[]{:T(128)} %convert_element_type.31, () %tuple.30, (s32[32]{0:T(128)S(1)}, s32[16384]{0:T(1024)S(1)}, bf16[64,8,128]{2,0,1:T(8,128)(2,1)S(1)}, bf16[16384,2,128]{2,1,0:T(2,128)(2,1)}, bf16[16384,2,128]{2,0,1:T(8,128)(2,1)}) %tuple.31), branch_computations={%region_6.7_spmd, %region_7.10_spmd} | conditional | flops 2173207296 | bytes 68824208 | solution.py:74
  333.3 0.3 broadcast_compare_fusion.1
  333.7 16.1 %fusion.31 = (f32[32,2,4]{0,2,1:T(4,128)S(1)}, f32[32,2,4,16384]{3,0,2,1:T(8,128)}) fusion(bf16[32,2,4,128]{3,0,2,1:T(8,128)(2,1)S(1)} %bitcast.54, bf16[16384,2,128,1]{2,1,0,3:T(2,128)(2,1)} %bitcast.57, pred[32,16384]{1,0:T(8,128)(4,1)S(1)} %broadcast_compare_fusion.1), kind=kOutput, calls=%fused_computation.49 | convolution fusion | flops 1086324480 | bytes 25756672 | tf_op jit(solution)/shard_map/cond/branch_1_fun/sjgd,tjd->sjgt/dot_general | solution.py:30
  349.8 8.1 %fusion.17 = f32[32,2,4]{0,2,1:T(4,128)S(1)} fusion(f32[32,2,4,16384]{3,0,2,1:T(8,128)} %get-tuple-element.77, f32[32,2,4]{0,2,1:T(4,128)S(1)} %broadcast_maximum_fusion.1), kind=kLoop, calls=%fused_computation.20 | loop fusion | flops 8388352 | bytes 16779264 | tf_op jit(solution)/shard_map/cond/branch_1_fun/reduce_sum | solution.py:38
  358.0 11.0 %fusion.24 = f32[32,2,4,128]{3,0,2,1:T(8,128)S(1)} fusion(bf16[16384,2,128]{2,0,1:T(8,128)(2,1)} %get-tuple-element.35, f32[32,2,4,16384]{3,0,2,1:T(8,128)} %get-tuple-element.77, f32[32,2,4]{0,2,1:T(4,128)S(1)} %broadcast_maximum_fusion.1, f32[32,2,4]{0,2,1:T(4,128)S(1)} %get-tuple-element.74), kind=kOutput, calls=%fused_computation.25 | convolution fusion | flops 1077968896 | bytes 25298944 | tf_op jit(solution)/shard_map/cond/branch_1_fun/sjgt,tjd->sjgd/dot_general | solution.py:39
  369.0 0.1 copy.29
  369.1 0.1 pad_maximum_fusion.2
  369.1 0.1 copy.16
  369.2 0.1 fusion.28
  369.4 5.7 %all_to_all.18 = bf16[64,8,128]{2,1,0:T(8,128)(2,1)S(1)} all-to-all(bf16[64,8,128]{2,1,0:T(8,128)(2,1)S(1)} %fusion.28), channel_id=1, replica_groups=mesh['ctx'=256,'tp'=2] {'tp'}, dimensions={0} | all-to-all | bytes 262144 | tf_op jit(solution)/shard_map/all_to_all | solution.py:105
  375.1 0.7 copy.40
  (10 shorter events, 0.1 us)
Async XLA Ops:
  7.2 150.5 %all-gather.5.cloned.1.call-start = ((), (), s32[]{:S(2)}) async-start(), calls=%async_computation.2 | async-start | bytes 8421376 | tf_op jit(solution)/shard_map/all_gather | solution.py:97
  8.6 288.8 %all-gather.3.cloned.1.call-start = ((), (), s32[]{:S(2)}) async-start(), calls=%async_computation.1 | async-start | bytes 8421376 | tf_op jit(solution)/shard_map/all_gather | solution.py:96
Sparse Core Ops, SparseCore 0:
  13.1 144.5 all-gather.4
  162.9 134.4 all-gather.2
where the time goes:
time: 383 us
  waiting for transfers between devices  284 us (74%)
  matrix products  54.2 us (14%)
  other arithmetic  21.1 us (6%)
  between operations  15.4 us (4%)
  blocking collectives  5.7 us (1%)
    all_gather x1, waiting for transfers between devices, per_device(): lax.all_gather(incoming_content_vectors, 'ctx', axis=0, tiled=True)  144 us
    all_gather x1, waiting for transfers between devices, per_device(): lax.all_gather(key_cache, 'ctx', axis=0, tiled=True)  140 us
    dot_general x2, matrix products, absorb(): jnp.einsum('sjgd,tjd->sjgt', q_block, key_piece, preferred_element_type=j...  32.2 us
    dot_general x2, matrix products, absorb(): jnp.einsum('sjgt,tjd->sjgd', weights, value_piece.astype(jnp.float32))  22 us
    reduce_sum x2, other arithmetic, absorb(): new_sum = factor * run_sum + jnp.sum(weights, axis=-1)  16.3 us
  transfers between devices with their start and end apart: 2, of which 2 were waited for; matrix products, arithmetic and copies ran while one was open for 1% of the time, Pallas kernels for 0%

commit v1 on v0

v1 whole, which is shorter than its diff:
```python
import functools
import math

import jax
import jax.numpy as jnp
from jax import lax
from jax.experimental import pallas as pl
from jax.experimental.pallas import tpu as pltpu
from jax.sharding import PartitionSpec as P

MESH = pl.DeviceIdType.MESH
rope_base = 500000.0
RING = 8
CELLS = RING * RING
HALF = 64
PIECE = 2 * HALF
WIDTH = 128
GROUP = 4
ROWS = GROUP * PIECE
LAG = 2


def rotate(tensor, positions):
    feature_width = tensor.shape[-1]
    half_width = feature_width // 2
    inverse_freq = rope_base ** (-(jnp.arange(half_width, dtype=jnp.float32) * 2.0 / feature_width))
    angles = positions.astype(jnp.float32)[:, None] * inverse_freq[None, :]
    cosine = jnp.cos(angles)[:, None, :]
    sine_part = jnp.sin(angles)[:, None, :]
    widened = tensor.astype(jnp.float32)
    front_half = widened[..., :half_width]
    second = widened[..., half_width:]
    return jnp.concatenate(
        [front_half * cosine - second * sine_part, second * cosine + front_half * sine_part],
        axis=-1,
    ).astype(jnp.bfloat16)


def offset_of(k):
    return ((k + 1) // 2) * (1 - 2 * (k % 2))


def event_order():
    entries = [(i, 0, i) for i in range(1, 5)]
    for j in range(1, 4):
        for k in range(8):
            entries.append((j + abs(offset_of(k)), j, k))
    for k in range(4):
        entries.append((4 + abs(offset_of(2 * k + 1)), 4, k))
    entries.sort()
    return [(j, k) for _, j, k in entries]


ORDER = event_order()
EVENTS = len(ORDER)
PER_WORD = 5
WORDS = []
for first in range(0, EVENTS, PER_WORD):
    word = 0
    for place, (j, k) in enumerate(ORDER[first : first + PER_WORD]):
        word |= (j * 8 + k) << (6 * place)
    WORDS.append(word)


def decode(n):
    which = n // PER_WORD
    word = jnp.int32(WORDS[0])
    for at in range(1, len(WORDS)):
        word = jnp.where(which == at, jnp.int32(WORDS[at]), word)
    code = lax.shift_right_logical(word, 6 * (n - which * PER_WORD)) & 63
    j = code // 8
    k = code % 8
    first = j == 0
    last = j == 4
    odd = k % 2
    kl = jnp.where(first, 2 * k - 1, jnp.where(last, 2 * k + odd, k))
    kr = jnp.where(first, 2 * k, jnp.where(last, 2 * k + 1 - odd, k))
    return j, k, kl, kr


def kernel(q_ref, kv_ref, out_ref, buf, qbuf, obuf, acc, top, send_sem, own_sem, other_sem, swap_send, swap_recv, out_send, out_recv):
    ctx = lax.axis_index("ctx")
    tp = lax.axis_index("tp")
    core = ctx % 2
    xh = (ctx // 2) % 2
    cell = ctx // 4
    y = cell % RING
    z = cell // RING
    zfirst = core == 0
    my_a = jnp.where(zfirst, z, y)
    my_b = jnp.where(zfirst, y, z)
    stride_a = jnp.where(zfirst, RING, 1)
    stride_b = jnp.where(zfirst, 1, RING)

    def cell_at(a, b):
        return ((a + 2 * RING) % RING) * stride_a + ((b + 2 * RING) % RING) * stride_b

    def other_cell_at(a, b):
        return ((a + 2 * RING) % RING) * stride_b + ((b + 2 * RING) % RING) * stride_a

    def dev(at):
        return (at * 4 + xh * 2 + core, tp)

    a_up, a_down = dev(cell_at(my_a + 1, my_b)), dev(cell_at(my_a - 1, my_b))
    b_up, b_down = dev(cell_at(my_a, my_b + 1)), dev(cell_at(my_a, my_b - 1))
    mate = (cell * 4 + xh * 2 + 1 - core, tp)
    swap = (cell * 4 + (1 - xh) * 2 + core, tp)
    side = (ctx, 1 - tp)
    cross = (cell * 4 + (1 - xh) * 2 + core, 1 - tp)

    barrier = pltpu.get_barrier_semaphore()
    for device in (a_up, a_down, b_up, b_down, mate, swap, side, cross):
        pl.semaphore_signal(barrier, inc=1, device_id=device, device_id_type=MESH)
    pl.semaphore_wait(barrier, 8)

    mine = core * CELLS
    theirs = (1 - core) * CELLS
    own = mine + cell
    keep_rows = pl.ds(pl.multiple_of(xh * HALF, HALF), HALF)
    get_rows = pl.ds(pl.multiple_of((1 - xh) * HALF, HALF), HALF)

    def remote(src, dst, s_sem, r_sem, device):
        return pltpu.make_async_remote_copy(
            src_ref=src, dst_ref=dst, send_sem=s_sem, recv_sem=r_sem, device_id=device, device_id_type=MESH
        )

    kv_out = remote(kv_ref.at[1 - xh], buf.at[own, keep_rows], swap_send.at[0], swap_recv.at[0], swap)
    kv_out.start()
    ring_targets = (a_up, a_down, b_up, b_down)
    for device in ring_targets:
        remote(kv_ref.at[xh], buf.at[own, keep_rows], send_sem, own_sem.at[cell], device).start()
    remote(kv_ref.at[xh], buf.at[own, keep_rows], send_sem, other_sem.at[cell], mate).start()
    other_heads = pl.ds(pl.multiple_of((1 - xh) * GROUP, GROUP), GROUP)
    own_heads = pl.ds(pl.multiple_of(xh * GROUP, GROUP), GROUP)
    q_out = remote(q_ref.at[other_heads], qbuf.at[:, xh], swap_send.at[1], swap_recv.at[1], swap)
    q_out.start()
    buf[own, keep_rows] = kv_ref[xh]
    qbuf[:, xh] = q_ref[own_heads]

    remote(kv_ref.at[1 - xh], buf.at[own, get_rows], swap_send.at[0], swap_recv.at[0], swap).wait_recv()
    for device in ring_targets:
        remote(buf.at[own, get_rows], buf.at[own, get_rows], send_sem, own_sem.at[cell], device).start()
    remote(buf.at[own, get_rows], buf.at[own, get_rows], send_sem, other_sem.at[cell], mate).start()
    remote(q_ref.at[other_heads], qbuf.at[:, 1 - xh], swap_send.at[1], swap_recv.at[1], swap).wait_recv()

    factor = math.log2(math.e) / math.sqrt(WIDTH)

    def pass_on(at, device):
        spot = buf.at[mine + at]
        remote(spot, spot, send_sem, own_sem.at[at], device).start()

    def share(at):
        spot = buf.at[mine + at]
        remote(spot, spot, send_sem, other_sem.at[at], mate).start()

    def wait_own(at):
        spot = buf.at[mine + at]
        remote(spot, spot, send_sem, own_sem.at[at], b_up).wait_recv()

    def wait_other(at):
        spot = buf.at[theirs + at]
        remote(spot, spot, send_sem, other_sem.at[at], mate).wait_recv()

    def scores_of(keys):
        q = qbuf[...].reshape(ROWS, WIDTH)
        return lax.dot_general(q, keys, (((1,), (1,)), ((), ())), preferred_element_type=jnp.float32) * factor

    def row_max(parts):
        most = parts[0]
        for part in parts[1:]:
            most = jnp.maximum(most, part)
        return jnp.broadcast_to(jnp.max(most, axis=1, keepdims=True), (ROWS, WIDTH))

    wait_other(cell)
    row = lax.broadcasted_iota(jnp.int32, (ROWS, WIDTH), 0) % PIECE
    col = lax.broadcasted_iota(jnp.int32, (ROWS, WIDTH), 1)
    row_at = jnp.where(row < HALF, row, row + HALF) + core * HALF
    parts = []
    for piece, which in ((own, core), (theirs + cell, 1 - core)):
        col_at = jnp.where(col < HALF, col, col + HALF) + which * HALF
        s = scores_of(buf[piece, :, :WIDTH])
        parts.append(jnp.where(row_at >= col_at, s, -jnp.inf))
    most = row_max(parts)
    top[...] = most
    ones = jnp.ones((PIECE, WIDTH), jnp.bfloat16)
    total = None
    for part, piece in zip(parts, (own, theirs + cell)):
        p = jnp.exp2(part - most).astype(jnp.bfloat16)
        v = jnp.concatenate([buf[piece, :, WIDTH:], ones], axis=1)
        term = jnp.dot(p, v, preferred_element_type=jnp.float32)
        total = term if total is None else total + term
    acc[...] = total

    def attend(pieces):
        some = pieces[0][1]
        spare = pieces[0][0]
        for piece, valid in pieces[1:]:
            spare = jnp.where(some, spare, piece)
            some = jnp.logical_or(some, valid)

        @pl.when(some)
        def _():
            keys, values = [], []
            for piece, valid in pieces:
                at = jnp.where(valid, piece, spare)
                weight = jnp.full((PIECE, WIDTH), jnp.where(valid, 1.0, 0.0), jnp.float32).astype(jnp.bfloat16)
                keys.append(buf[at, :, :WIDTH])
                values.append(jnp.concatenate([buf[at, :, WIDTH:] * weight, weight], axis=1))
            s = scores_of(jnp.concatenate(keys, axis=0))
            parts = [s[:, at * WIDTH : (at + 1) * WIDTH] for at in range(len(pieces))]
            old = top[...]
            new = jnp.maximum(old, row_max(parts))
            top[...] = new
            shrink = jnp.exp2(old - new)
            p = jnp.concatenate([jnp.exp2(part - new).astype(jnp.bfloat16) for part in parts], axis=1)
            fresh = jnp.dot(p, jnp.concatenate(values, axis=0), preferred_element_type=jnp.float32)
            acc[:, :WIDTH] = acc[:, :WIDTH] * shrink + fresh[:, :WIDTH]
            acc[:, WIDTH:] = acc[:, WIDTH:] * shrink + fresh[:, WIDTH:]

    def step(n, carry):
        now = jnp.minimum(n, EVENTS - 1)
        live = n < EVENTS
        j, k, kl, kr = decode(now)
        left = cell_at(my_a + offset_of(kl), my_b - j)
        right = cell_at(my_a + offset_of(kr), my_b + j)
        both = kr < 8

        @pl.when(jnp.logical_and(live, j == 0))
        def _():
            wait_own(left)

            @pl.when(k < 4)
            def _():
                pass_on(left, a_up)

            pass_on(left, b_up)
            pass_on(left, b_down)
            share(left)

            @pl.when(k < 4)
            def _():
                wait_own(right)

                @pl.when(k < 3)
                def _():
                    pass_on(right, a_down)

                pass_on(right, b_up)
                pass_on(right, b_down)
                share(right)

        @pl.when(jnp.logical_and(live, j > 0))
        def _():
            wait_own(left)

            @pl.when(jnp.logical_or(j < 3, jnp.logical_and(j == 3, kl % 2 == (kl // 2) % 2)))
            def _():
                pass_on(left, b_up)

            share(left)
            wait_own(right)

            @pl.when(jnp.logical_or(j < 3, jnp.logical_and(j == 3, kr % 2 != (kr // 2) % 2)))
            def _():
                pass_on(right, b_down)

            share(right)

        past = jnp.maximum(n - LAG, 0)
        due = n >= LAG
        j2, k2, kl2, kr2 = decode(past)
        left2 = other_cell_at(my_b + offset_of(kl2), my_a - j2)
        right2 = other_cell_at(my_b + offset_of(kr2), my_a + j2)
        both2 = kr2 < 8

        @pl.when(due)
        def _():
            wait_other(left2)

            @pl.when(both2)
            def _():
                wait_other(right2)

        attend(
            [
                (mine + left, jnp.logical_and(live, left < cell)),
                (mine + right, jnp.logical_and(jnp.logical_and(live, both), right < cell)),
                (theirs + left2, jnp.logical_and(due, left2 < cell)),
                (theirs + right2, jnp.logical_and(jnp.logical_and(due, both2), right2 < cell)),
            ]
        )
        return carry

    lax.fori_loop(0, EVENTS + LAG, step, 0)

    o = (acc[:, :WIDTH] / acc[:, WIDTH:]).astype(jnp.bfloat16)
    obuf[...] = o.reshape(GROUP, 2, 2, HALF // 2, WIDTH)
    heads = pl.ds(pl.multiple_of(tp * 8 + xh * 4, 4), GROUP)
    places = ((xh, 1 - tp, side), (1 - xh, tp, swap), (1 - xh, 1 - tp, cross))
    for at, (to_xh, to_tp, device) in enumerate(places):
        remote(obuf.at[:, to_xh, to_tp], out_ref.at[heads], out_send.at[at], out_recv.at[at], device).start()
    out_ref[heads] = obuf[:, xh, tp]
    for at, (to_xh, to_tp, device) in enumerate(places):
        from_heads = pl.ds(pl.multiple_of(to_tp * 8 + to_xh * 4, 4), GROUP)
        remote(obuf.at[:, to_xh, to_tp], out_ref.at[from_heads], out_send.at[at], out_recv.at[at], device).wait()

    kv_out.wait_send()
    q_out.wait_send()
    everything = buf.at[pl.ds(0, 127)]
    remote(everything, everything, send_sem, own_sem.at[cell], b_up).wait_send()


def per_device(queries, incoming_lookup_vectors, incoming_content_vectors):
    tok_rows = queries.shape[0]
    my_index = lax.axis_index("ctx")
    natural_pos = my_index * tok_rows + jnp.arange(tok_rows, dtype=jnp.int32)
    key_cache = rotate(incoming_lookup_vectors, natural_pos)
    spun = rotate(queries, natural_pos).transpose(1, 0, 2)
    pair = jnp.concatenate([key_cache, incoming_content_vectors], axis=-1).transpose(1, 0, 2)
    vmem = pl.BlockSpec(memory_space=pltpu.VMEM)
    out = pl.pallas_call(
        kernel,
        out_shape=jax.ShapeDtypeStruct((16, HALF // 2, WIDTH), jnp.bfloat16),
        in_specs=[vmem, vmem],
        out_specs=vmem,
        scratch_shapes=[
            pltpu.VMEM((2 * CELLS, PIECE, 2 * WIDTH), jnp.bfloat16),
            pltpu.VMEM((GROUP, 2, HALF, WIDTH), jnp.bfloat16),
            pltpu.VMEM((GROUP, 2, 2, HALF // 2, WIDTH), jnp.bfloat16),
            pltpu.VMEM((ROWS, 2 * WIDTH), jnp.float32),
            pltpu.VMEM((ROWS, WIDTH), jnp.float32),
            pltpu.SemaphoreType.DMA,
            pltpu.SemaphoreType.DMA((CELLS,)),
            pltpu.SemaphoreType.DMA((CELLS,)),
            pltpu.SemaphoreType.DMA((2,)),
            pltpu.SemaphoreType.DMA((2,)),
            pltpu.SemaphoreType.DMA((3,)),
            pltpu.SemaphoreType.DMA((3,)),
        ],
        compiler_params=pltpu.CompilerParams(
            collective_id=0, has_side_effects=True, vmem_limit_bytes=48 * 1024 * 1024
        ),
        name="cell_attention",
    )(spun, pair)
    return (out.transpose(1, 0, 2), key_cache)


def solution(mesh):
    return jax.shard_map(
        per_device,
        mesh=mesh,
        in_specs=(P("ctx", "tp", None), P("ctx", "tp", None), P("ctx", "tp", None)),
        out_specs=(P(("ctx", "tp"), None, None), P("ctx", "tp", None)),
        check_vma=False,
    )
```

time: 383 us -> 62.6 us (0.16)
  the two profiles are of different devices: /device:TPU:1 before, /device:TPU:8 now
where the time goes in v1:
time: 62.6 us; the launch traced here: 62.4 us
  Pallas kernels  57.3 us (92%)
  local copies, waits for them, and re-layouts  2.75 us (4%)
  other arithmetic  1.66 us (3%)
  between operations  0.71 us (1%)
    pallas_call x1, Pallas kernels, per_device(): pl.pallas_call(kernel, out_shape=jax.ShapeDtypeStruct((16, HALF // 2, WID...  57.3 us
    unnamed x7, local copies, waits for them, and re-layouts  2.75 us

profile of v1, /device:TPU:8, one launch (start us, length us, event | category | flops | bytes accessed | tf_op | source)
XLA Modules:
  0.0 62.4 jit_solution(17775020868647135373)
XLA Ops:
  0.6 0.9 %copy_convert_fusion = f32[64,8,128]{2,0,1:T(8,128)S(1)} fusion(bf16[64,8,128]{2,1,0:T(8,128)(2,1)} %param.3), kind=kLoop, calls=%fused_computation.3 | loop fusion | flops 65536 | bytes 393216 | tf_op jit(solution)/shard_map/convert_element_type | solution.py:30
  1.6 0.2 multiply_cosine_fusion
  1.8 0.2 subtract_convert_fusion
  1.9 0.0 copy-start.1
  2.0 0.1 maximum_bitcast_fusion.q_ref
  2.1 0.6 %copy-done.1 = bf16[64,2,128]{2,1,0:T(2,128)(2,1)S(1)} copy-done((bf16[64,2,128]{2,1,0:T(2,128)(2,1)S(1)}, bf16[64,2,128]{2,1,0:T(2,128)(2,1)}, u32[]{:S(2)}) %copy-start.1) | copy-done | bytes 32792
  2.7 0.0 copy-start
  2.7 0.7 %copy-done = bf16[64,2,128]{2,1,0:T(2,128)(2,1)S(1)} copy-done((bf16[64,2,128]{2,1,0:T(2,128)(2,1)S(1)}, bf16[64,2,128]{2,1,0:T(2,128)(2,1)}, u32[]{:S(2)}) %copy-start) | copy-done | bytes 32792
  3.5 0.1 subtract_convert_fusion.1
  3.6 0.1 maximum_bitcast_fusion.1.kv_ref
  3.7 57.3 %cell_attention.1 = bf16[16,32,128]{2,1,0:T(8,128)(2,1)S(1)} custom-call(bf16[8,64,128]{2,1,0:T(8,128)(2,1)S(1)} %maximum_bitcast_fusion.q_ref, bf16[2,64,256]{2,1,0:T(8,128)(2,1)S(1)} %maximum_bitcast_fusion.1.kv_ref), custom_call_target="tpu_custom_call" | custom-call | tf_op jit(solution)/shard_map/cell_attention/pallas_call | solution.py:321
  60.9 0.7 %copy.8 = bf16[32,16,128]{2,1,0:T(8,128)(2,1)} copy(bf16[32,16,128]{2,0,1:T(8,128)(2,1)S(1)} %bitcast.5) | data formatting | bytes 262144
  61.6 0.1 pad_maximum_fusion
  61.7 0.6 %copy.9 = bf16[64,2,128]{2,1,0:T(2,128)(2,1)} copy(bf16[64,2,128]{2,0,1:T(8,128)(2,1)S(1)} %pad_maximum_fusion) | data formatting | bytes 65536
  (4 shorter events, 0.0 us)
Async XLA Ops:
  1.9 0.8 %copy-start.1 = (bf16[64,2,128]{2,1,0:T(2,128)(2,1)S(1)}, bf16[64,2,128]{2,1,0:T(2,128)(2,1)}, u32[]{:S(2)}) copy-start(bf16[64,2,128]{2,1,0:T(2,128)(2,1)} %param.5) | copy-start | bytes 98308
  2.7 0.8 %copy-start = (bf16[64,2,128]{2,1,0:T(2,128)(2,1)S(1)}, bf16[64,2,128]{2,1,0:T(2,128)(2,1)}, u32[]{:S(2)}) copy-start(bf16[64,2,128]{2,1,0:T(2,128)(2,1)} %param.4) | copy-start | bytes 98308

commit v2 on v0

v2 whole, which is shorter than its diff:
```python
import functools
import math

import jax
import jax.numpy as jnp
from jax import lax
from jax.experimental import pallas as pl
from jax.experimental.pallas import tpu as pltpu
from jax.sharding import PartitionSpec as P

MESH = pl.DeviceIdType.MESH
rope_base = 500000.0
RING = 8
CELLS = RING * RING
HALF = 64
PIECE = 2 * HALF
WIDTH = 128
GROUP = 4
ROWS = GROUP * PIECE
BATCH = 2


def rotate(tensor, positions):
    feature_width = tensor.shape[-1]
    half_width = feature_width // 2
    inverse_freq = rope_base ** (-(jnp.arange(half_width, dtype=jnp.float32) * 2.0 / feature_width))
    angles = positions.astype(jnp.float32)[:, None] * inverse_freq[None, :]
    cosine = jnp.cos(angles)[:, None, :]
    sine_part = jnp.sin(angles)[:, None, :]
    widened = tensor.astype(jnp.float32)
    front_half = widened[..., :half_width]
    second = widened[..., half_width:]
    return jnp.concatenate(
        [front_half * cosine - second * sine_part, second * cosine + front_half * sine_part],
        axis=-1,
    ).astype(jnp.bfloat16)


def offset_of(k):
    return ((k + 1) // 2) * (1 - 2 * (k % 2))


def far_left(k):
    return 4 if k in (0, 3, 4, 7) else 3


def far_right(k):
    return 7 - far_left(k)


def event_order():
    entries = [(i, 0, 2 * i - 1, 2 * i if i < 4 else None) for i in range(1, 5)]
    for j in range(1, 4):
        for k in range(8):
            entries.append((j + abs(offset_of(k)), j, k, k))
    for left, right in ((0, 1), (3, 2), (4, 5), (7, 6)):
        entries.append((4 + max(abs(offset_of(left)), abs(offset_of(right))), 4, left, right))
    entries.sort(key=lambda e: e[:3])
    return [e[1:] for e in entries]


ORDER = event_order()
SENDS = 8 * len(ORDER)


def kernel(q_ref, kv_ref, out_ref, buf, qbuf, obuf, acc, top, first_send, send_sem, own_sem, other_sem, swap_send, swap_recv, out_send, out_recv):
    ctx = lax.axis_index("ctx")
    tp = lax.axis_index("tp")
    core = ctx % 2
    xh = (ctx // 2) % 2
    cell = ctx // 4
    y = cell % RING
    z = cell // RING
    zfirst = core == 0

    def pick(flag, one, two):
        return jnp.where(flag, jnp.int32(one), jnp.int32(two))

    def pick_flag(flag, one, two):
        return pick(flag, one, two) != 0

    def cell_at(dz, dy):
        return ((z + dz + RING) % RING) * RING + (y + dy + RING) % RING

    def dev(at):
        return (at * 4 + xh * 2 + core, tp)

    steps = pick(zfirst, 1, 0)
    a_up = dev(cell_at(steps, 1 - steps))
    a_down = dev(cell_at(-steps, steps - 1))
    b_up = dev(cell_at(1 - steps, steps))
    b_down = dev(cell_at(steps - 1, -steps))
    mate = (cell * 4 + xh * 2 + 1 - core, tp)
    swap = (cell * 4 + (1 - xh) * 2 + core, tp)
    side = (ctx, 1 - tp)
    cross = (cell * 4 + (1 - xh) * 2 + core, 1 - tp)

    barrier = pltpu.get_barrier_semaphore()
    for device in (a_up, a_down, b_up, b_down, mate, swap, side, cross):
        pl.semaphore_signal(barrier, inc=1, device_id=device, device_id_type=MESH)
    pl.semaphore_wait(barrier, 8)

    mine = core * CELLS
    theirs = (1 - core) * CELLS
    own = mine + cell
    keep_rows = pl.ds(pl.multiple_of(xh * HALF, HALF), HALF)
    get_rows = pl.ds(pl.multiple_of((1 - xh) * HALF, HALF), HALF)

    def remote(src, dst, s_sem, r_sem, device):
        return pltpu.make_async_remote_copy(
            src_ref=src, dst_ref=dst, send_sem=s_sem, recv_sem=r_sem, device_id=device, device_id_type=MESH
        )

    kv_out = remote(kv_ref.at[1 - xh], buf.at[own, keep_rows], swap_send.at[0], swap_recv.at[0], swap)
    kv_out.start()
    below_top = z < RING - 1
    low = z < 3
    first_targets = (
        (a_up, pick_flag(zfirst, below_top, True)),
        (a_down, pick_flag(zfirst, low, True)),
        (b_up, pick_flag(zfirst, True, below_top)),
        (b_down, pick_flag(zfirst, True, low)),
    )

    def first_copies(src, part):
        for at, (device, needed) in enumerate(first_targets):
            yield needed, remote(src, buf.at[own, part], first_send.at[at], own_sem.at[cell], device)
        yield None, remote(src, buf.at[own, part], first_send.at[4], other_sem.at[cell], mate)

    def start_first(src, part):
        for needed, copy in first_copies(src, part):
            if needed is None:
                copy.start()
            else:
                pl.when(needed)(copy.start)

    start_first(kv_ref.at[xh], keep_rows)
    other_heads = pl.ds(pl.multiple_of((1 - xh) * GROUP, GROUP), GROUP)
    own_heads = pl.ds(pl.multiple_of(xh * GROUP, GROUP), GROUP)
    q_out = remote(q_ref.at[other_heads], qbuf.at[:, xh], swap_send.at[1], swap_recv.at[1], swap)
    q_out.start()
    buf[own, keep_rows] = kv_ref[xh]
    qbuf[:, xh] = q_ref[own_heads]

    remote(kv_ref.at[1 - xh], buf.at[own, get_rows], swap_send.at[0], swap_recv.at[0], swap).wait_recv()
    start_first(buf.at[own, get_rows], get_rows)
    remote(q_ref.at[other_heads], qbuf.at[:, 1 - xh], swap_send.at[1], swap_recv.at[1], swap).wait_recv()

    def piece_of(event, right, first_z):
        j, kl, kr = event
        k = kr if right else kl
        if k is None:
            return None
        along = offset_of(k)
        across = j if right else -j
        zz = (z + pick(first_z, along, across) + RING) % RING
        yy = (y + pick(first_z, across, along) + RING) % RING
        at = zz * RING + yy
        if j == 0:
            comes = pick_flag(first_z, zz < (3 if right else z), True)
        else:
            comes = pick_flag(first_z, zz <= z, zz < (far_right(k) if right else z))
        return at, comes, at < cell, zz

    def routes(event, right):
        j, kl, kr = event
        k = kr if right else kl
        zz = piece_of(event, right, zfirst)[3]
        if j == 0:
            ring_end = k >= (5 if right else 7)
            if not ring_end:
                yield (a_down if right else a_up), pick_flag(zfirst, True if right else below_top, True)
            yield b_up, pick_flag(zfirst, zz < z, below_top)
            yield b_down, pick_flag(zfirst, zz < z, z < far_right(k))
        elif right:
            if j < far_right(k):
                yield b_down, None
        elif j < far_left(k):
            yield b_up, pick_flag(zfirst, True, below_top)

    def copies(n, right):
        event = ORDER[n]
        at, _, seen, _ = piece_of(event, right, zfirst)
        spot = buf.at[mine + at]
        base = n * 8 + (4 if right else 0)
        yield seen, remote(spot, spot, send_sem.at[base], other_sem.at[at], mate)
        for place, (device, needed) in enumerate(routes(event, right)):
            yield needed, remote(spot, spot, send_sem.at[base + 1 + place], own_sem.at[at], device)

    def each_side(n, act):
        for right in (False, True):
            found = piece_of(ORDER[n], right, zfirst)
            if found is None:
                continue

            @pl.when(found[1])
            def _():
                act(n, right, found[0])

    def take(n, right, at):
        spot = buf.at[mine + at]
        remote(spot, spot, send_sem.at[0], own_sem.at[at], b_up).wait_recv()
        for needed, copy in copies(n, right):
            if needed is None:
                copy.start()
            else:
                pl.when(needed)(copy.start)

    def finish(n, right, at):
        for needed, copy in copies(n, right):
            if needed is None:
                copy.wait_send()
            else:
                pl.when(needed)(copy.wait_send)

    def wait_other(at):
        spot = buf.at[theirs + at]
        remote(spot, spot, send_sem.at[0], other_sem.at[at], mate).wait_recv()

    factor = math.log2(math.e) / math.sqrt(WIDTH)

    def scores_of(keys):
        q = qbuf[...].reshape(ROWS, WIDTH)
        return lax.dot_general(keys, q, (((1,), (1,)), ((), ())), preferred_element_type=jnp.float32)

    def weigh(values, p):
        return lax.dot_general(
            values, p.astype(jnp.bfloat16), (((0,), (0,)), ((), ())), preferred_element_type=jnp.float32
        )

    wait_other(cell)
    key = lax.broadcasted_iota(jnp.int32, (PIECE, ROWS), 0)
    row = lax.broadcasted_iota(jnp.int32, (PIECE, ROWS), 1) % PIECE
    row_at = jnp.where(row < HALF, row, row + HALF) + core * HALF
    key_at = jnp.where(key < HALF, key, key + HALF)
    both = (own, theirs + cell)
    s = scores_of(jnp.concatenate([buf[piece, :, :WIDTH] for piece in both], axis=0))
    s = jnp.concatenate(
        [
            jnp.where(row_at >= key_at + core * HALF, s[:PIECE], -1e30),
            jnp.where(row_at >= key_at + (1 - core) * HALF, s[PIECE:], -1e30),
        ],
        axis=0,
    )
    most = jnp.max(s, axis=0, keepdims=True)
    top[0:1] = most
    p = jnp.exp2((s - most) * factor)
    acc[WIDTH : WIDTH + 1] = jnp.sum(p, axis=0, keepdims=True)
    acc[:WIDTH] = weigh(jnp.concatenate([buf[piece, :, WIDTH:] for piece in both], axis=0), p)

    def attend(pieces):
        some = pieces[0][1]
        for _, seen in pieces[1:]:
            some = jnp.logical_or(some, seen)

        @pl.when(some)
        def _():
            spots = [jnp.where(seen, piece, own) for piece, seen in pieces]
            hide = [jnp.where(seen, 0.0, 1e30) for _, seen in pieces]
            s = scores_of(jnp.concatenate([buf[at, :, :WIDTH] for at in spots], axis=0))
            parts = [s[at * PIECE : (at + 1) * PIECE] for at in range(len(pieces))]
            old = top[0:1]
            new = old
            for part, away in zip(parts, hide):
                new = jnp.maximum(new, jnp.max(part, axis=0, keepdims=True) - away)
            top[0:1] = new
            shrink = jnp.exp2((old - new) * factor)
            p = jnp.concatenate([jnp.exp2((part - (new + away)) * factor) for part, away in zip(parts, hide)], axis=0)
            fresh = weigh(jnp.concatenate([buf[at, :, WIDTH:] for at in spots], axis=0), p)
            acc[WIDTH : WIDTH + 1] = acc[WIDTH : WIDTH + 1] * shrink + jnp.sum(p, axis=0, keepdims=True)
            acc[:WIDTH] = acc[:WIDTH] * shrink + fresh

    events = len(ORDER)
    for start in range(0, events + BATCH, BATCH):
        pieces = []
        for n in range(start, start + BATCH):
            if n < events:
                each_side(n, take)
                for right in (False, True):
                    found = piece_of(ORDER[n], right, zfirst)
                    if found is not None:
                        pieces.append((mine + found[0], found[2]))
        for n in range(start - BATCH, start):
            if n >= 0:
                for right in (False, True):
                    found = piece_of(ORDER[n], right, jnp.logical_not(zfirst))
                    if found is not None:
                        pl.when(found[2])(functools.partial(wait_other, found[0]))
                        pieces.append((theirs + found[0], found[2]))
        attend(pieces)

    o = (acc[:WIDTH] / acc[WIDTH : WIDTH + 1]).T.astype(jnp.bfloat16)
    obuf[...] = o.reshape(GROUP, 2, 2, HALF // 2, WIDTH)
    heads = pl.ds(pl.multiple_of(tp * 8 + xh * 4, 4), GROUP)
    places = ((xh, 1 - tp, side), (1 - xh, tp, swap), (1 - xh, 1 - tp, cross))
    for at, (to_xh, to_tp, device) in enumerate(places):
        remote(obuf.at[:, to_xh, to_tp], out_ref.at[heads], out_send.at[at], out_recv.at[at], device).start()
    out_ref[heads] = obuf[:, xh, tp]
    kv_out.wait_send()
    q_out.wait_send()
    whole = buf.at[own]
    for at, (device, needed) in enumerate(first_targets):
        pl.when(needed)(remote(whole, whole, first_send.at[at], own_sem.at[cell], device).wait_send)
    remote(whole, whole, first_send.at[4], other_sem.at[cell], mate).wait_send()
    for n in range(events):
        each_side(n, finish)
    for at, (to_xh, to_tp, device) in enumerate(places):
        from_heads = pl.ds(pl.multiple_of(to_tp * 8 + to_xh * 4, 4), GROUP)
        remote(obuf.at[:, to_xh, to_tp], out_ref.at[from_heads], out_send.at[at], out_recv.at[at], device).wait()


def per_device(queries, incoming_lookup_vectors, incoming_content_vectors):
    tok_rows = queries.shape[0]
    my_index = lax.axis_index("ctx")
    natural_pos = my_index * tok_rows + jnp.arange(tok_rows, dtype=jnp.int32)
    key_cache = rotate(incoming_lookup_vectors, natural_pos)
    spun = rotate(queries, natural_pos).transpose(1, 0, 2)
    pair = jnp.concatenate([key_cache, incoming_content_vectors], axis=-1).transpose(1, 0, 2)
    vmem = pl.BlockSpec(memory_space=pltpu.VMEM)
    out = pl.pallas_call(
        kernel,
        out_shape=jax.ShapeDtypeStruct((16, HALF // 2, WIDTH), jnp.bfloat16),
        in_specs=[vmem, vmem],
        out_specs=vmem,
        scratch_shapes=[
            pltpu.VMEM((2 * CELLS, PIECE, 2 * WIDTH), jnp.bfloat16),
            pltpu.VMEM((GROUP, 2, HALF, WIDTH), jnp.bfloat16),
            pltpu.VMEM((GROUP, 2, 2, HALF // 2, WIDTH), jnp.bfloat16),
            pltpu.VMEM((WIDTH + 8, ROWS), jnp.float32),
            pltpu.VMEM((8, ROWS), jnp.float32),
            pltpu.SemaphoreType.DMA((5,)),
            pltpu.SemaphoreType.DMA((SENDS,)),
            pltpu.SemaphoreType.DMA((CELLS,)),
            pltpu.SemaphoreType.DMA((CELLS,)),
            pltpu.SemaphoreType.DMA((2,)),
            pltpu.SemaphoreType.DMA((2,)),
            pltpu.SemaphoreType.DMA((3,)),
            pltpu.SemaphoreType.DMA((3,)),
        ],
        compiler_params=pltpu.CompilerParams(
            collective_id=0, has_side_effects=True, vmem_limit_bytes=48 * 1024 * 1024
        ),
        name="cell_attention",
    )(spun, pair)
    return (out.transpose(1, 0, 2), key_cache)


def solution(mesh):
    return jax.shard_map(
        per_device,
        mesh=mesh,
        in_specs=(P("ctx", "tp", None), P("ctx", "tp", None), P("ctx", "tp", None)),
        out_specs=(P(("ctx", "tp"), None, None), P("ctx", "tp", None)),
        check_vma=False,
    )
```

time: 383 us -> 54.4 us (0.14)
  the two profiles are of different devices: /device:TPU:1 before, /device:TPU:448 now
where the time goes in v2:
time: 54.4 us; the launch traced here: 54.2 us
  Pallas kernels  49 us (90%)
  local copies, waits for them, and re-layouts  2.75 us (5%)
  other arithmetic  1.66 us (3%)
  between operations  0.71 us (1%)
    pallas_call x1, Pallas kernels, per_device(): pl.pallas_call(kernel, out_shape=jax.ShapeDtypeStruct((16, HALF // 2, WID...  49 us
    unnamed x7, local copies, waits for them, and re-layouts  2.75 us

profile of v2, /device:TPU:448, one launch (start us, length us, event | category | flops | bytes accessed | tf_op | source)
XLA Modules:
  0.0 54.2 jit_solution(7491247508590242650)
XLA Ops:
  0.6 0.9 %copy_convert_fusion = f32[64,8,128]{2,0,1:T(8,128)S(1)} fusion(bf16[64,8,128]{2,1,0:T(8,128)(2,1)} %param.3), kind=kLoop, calls=%fused_computation.3 | loop fusion | flops 65536 | bytes 393216 | tf_op jit(solution)/shard_map/convert_element_type | solution.py:30
  1.6 0.2 multiply_cosine_fusion
  1.8 0.2 subtract_convert_fusion
  1.9 0.0 copy-start.1
  2.0 0.1 maximum_bitcast_fusion.q_ref
  2.1 0.6 %copy-done.1 = bf16[64,2,128]{2,1,0:T(2,128)(2,1)S(1)} copy-done((bf16[64,2,128]{2,1,0:T(2,128)(2,1)S(1)}, bf16[64,2,128]{2,1,0:T(2,128)(2,1)}, u32[]{:S(2)}) %copy-start.1) | copy-done | bytes 32792
  2.7 0.0 copy-start
  2.7 0.7 %copy-done = bf16[64,2,128]{2,1,0:T(2,128)(2,1)S(1)} copy-done((bf16[64,2,128]{2,1,0:T(2,128)(2,1)S(1)}, bf16[64,2,128]{2,1,0:T(2,128)(2,1)}, u32[]{:S(2)}) %copy-start) | copy-done | bytes 32792
  3.5 0.1 subtract_convert_fusion.1
  3.6 0.1 maximum_bitcast_fusion.1.kv_ref
  3.7 49.0 %cell_attention.1 = bf16[16,32,128]{2,1,0:T(8,128)(2,1)S(1)} custom-call(bf16[8,64,128]{2,1,0:T(8,128)(2,1)S(1)} %maximum_bitcast_fusion.q_ref, bf16[2,64,256]{2,1,0:T(8,128)(2,1)S(1)} %maximum_bitcast_fusion.1.kv_ref), custom_call_target="tpu_custom_call" | custom-call | tf_op jit(solution)/shard_map/cell_attention/pallas_call | solution.py:320
  52.7 0.7 %copy.8 = bf16[32,16,128]{2,1,0:T(8,128)(2,1)} copy(bf16[32,16,128]{2,0,1:T(8,128)(2,1)S(1)} %bitcast.5) | data formatting | bytes 262144
  53.4 0.1 pad_maximum_fusion
  53.5 0.6 %copy.9 = bf16[64,2,128]{2,1,0:T(2,128)(2,1)} copy(bf16[64,2,128]{2,0,1:T(8,128)(2,1)S(1)} %pad_maximum_fusion) | data formatting | bytes 65536
  (4 shorter events, 0.0 us)
Async XLA Ops:
  1.9 0.8 %copy-start.1 = (bf16[64,2,128]{2,1,0:T(2,128)(2,1)S(1)}, bf16[64,2,128]{2,1,0:T(2,128)(2,1)}, u32[]{:S(2)}) copy-start(bf16[64,2,128]{2,1,0:T(2,128)(2,1)} %param.5) | copy-start | bytes 98308
  2.7 0.8 %copy-start = (bf16[64,2,128]{2,1,0:T(2,128)(2,1)S(1)}, bf16[64,2,128]{2,1,0:T(2,128)(2,1)}, u32[]{:S(2)}) copy-start(bf16[64,2,128]{2,1,0:T(2,128)(2,1)} %param.4) | copy-start | bytes 98308

commit v3 on v2

--- a/solution.py
+++ b/solution.py
@@ -20,22 +20,6 @@
 BATCH = 2
 
 
-def rotate(tensor, positions):
-    feature_width = tensor.shape[-1]
-    half_width = feature_width // 2
-    inverse_freq = rope_base ** (-(jnp.arange(half_width, dtype=jnp.float32) * 2.0 / feature_width))
-    angles = positions.astype(jnp.float32)[:, None] * inverse_freq[None, :]
-    cosine = jnp.cos(angles)[:, None, :]
-    sine_part = jnp.sin(angles)[:, None, :]
-    widened = tensor.astype(jnp.float32)
-    front_half = widened[..., :half_width]
-    second = widened[..., half_width:]
-    return jnp.concatenate(
-        [front_half * cosine - second * sine_part, second * cosine + front_half * sine_part],
-        axis=-1,
-    ).astype(jnp.bfloat16)
-
-
 def offset_of(k):
     return ((k + 1) // 2) * (1 - 2 * (k % 2))
 
@@ -60,10 +44,55 @@
 
 
 ORDER = event_order()
-SENDS = 8 * len(ORDER)
-
-
-def kernel(q_ref, kv_ref, out_ref, buf, qbuf, obuf, acc, top, first_send, send_sem, own_sem, other_sem, swap_send, swap_recv, out_send, out_recv):
+EVENTS = len(ORDER)
+BATCHES = EVENTS // BATCH
+
+
+def landing_events():
+    found = {}
+    for n, (j, kl, kr) in enumerate(ORDER):
+        found[j, False, kl] = n
+        if kr is not None:
+            found[j, True, kr] = n
+    return found
+
+
+LANDING = landing_events()
+
+
+def sends_of(first_z, z, y):
+    top_row, low = z == RING - 1, z < 3
+    total = 1 + (not (first_z and top_row)) + (not first_z or low) + (first_z or not top_row) + (first_z or low)
+    for j, kl, kr in ORDER:
+        for right, k in ((False, kl), (True, kr)):
+            if k is None:
+                continue
+            along, across = offset_of(k), j if right else -j
+            zz = (z + (along if first_z else across)) % RING
+            yy = (y + (across if first_z else along)) % RING
+            if j == 0:
+                comes = zz < (3 if right else z) if first_z else True
+            else:
+                comes = zz <= z if first_z else zz < (far_right(k) if right else z)
+            if not comes:
+                continue
+            total += zz * RING + yy < z * RING + y
+            if j == 0:
+                if k < (5 if right else 7):
+                    total += not (first_z and not right and top_row)
+                total += zz < z if first_z else not top_row
+                total += zz < z if first_z else z < far_right(k)
+            elif right:
+                total += j < far_right(k)
+            elif j < far_left(k):
+                total += first_z or not top_row
+    return total
+
+
+TOTALS = sorted({sends_of(f, z, y) for f in (True, False) for z in range(RING) for y in range(RING)})
+
+
+def kernel(q_raw, k_raw, v_raw, cos_ref, sin_ref, out_ref, key_ref, q_ref, kv_ref, landed, buf, qbuf, obuf, acc, top, send_sem, own_sem, other_sem, swap_send, swap_recv, out_send, out_recv):
     ctx = lax.axis_index("ctx")
     tp = lax.axis_index("tp")
     core = ctx % 2
@@ -98,6 +127,20 @@
     barrier = pltpu.get_barrier_semaphore()
     for device in (a_up, a_down, b_up, b_down, mate, swap, side, cross):
         pl.semaphore_signal(barrier, inc=1, device_id=device, device_id_type=MESH)
+
+    cosine = cos_ref[...][:, None, :]
+    sine = sin_ref[...][:, None, :]
+
+    def rotated(raw):
+        wide = raw[...].astype(jnp.float32)
+        return wide * cosine + pltpu.roll(wide, WIDTH // 2, 2) * sine
+
+    keys = rotated(k_raw)
+    key_ref[...] = keys.astype(jnp.bfloat16)
+    kv_ref[:, :, :WIDTH] = jnp.swapaxes(keys, 0, 1).astype(jnp.bfloat16)
+    kv_ref[:, :, WIDTH:] = jnp.swapaxes(v_raw[...].astype(jnp.float32), 0, 1).astype(jnp.bfloat16)
+    q_ref[...] = jnp.swapaxes(rotated(q_raw), 0, 1).astype(jnp.bfloat16)
+
     pl.semaphore_wait(barrier, 8)
 
     mine = core * CELLS
@@ -122,17 +165,13 @@
         (b_down, pick_flag(zfirst, True, low)),
     )
 
-    def first_copies(src, part):
-        for at, (device, needed) in enumerate(first_targets):
-            yield needed, remote(src, buf.at[own, part], first_send.at[at], own_sem.at[cell], device)
-        yield None, remote(src, buf.at[own, part], first_send.at[4], other_sem.at[cell], mate)
+    first_sems = (LANDING[0, False, 1], LANDING[0, True, 2], LANDING[1, False, 0], LANDING[1, True, 0])
+    sent = [jnp.int32(1)] + [needed.astype(jnp.int32) for _, needed in first_targets]
 
     def start_first(src, part):
-        for needed, copy in first_copies(src, part):
-            if needed is None:
-                copy.start()
-            else:
-                pl.when(needed)(copy.start)
+        for at, (device, needed) in zip(first_sems, first_targets):
+            pl.when(needed)(remote(src, buf.at[own, part], send_sem, own_sem.at[at], device).start)
+        remote(src, buf.at[own, part], send_sem, other_sem.at[BATCHES], mate).start()
 
     start_first(kv_ref.at[xh], keep_rows)
     other_heads = pl.ds(pl.multiple_of((1 - xh) * GROUP, GROUP), GROUP)
@@ -169,53 +208,40 @@
         if j == 0:
             ring_end = k >= (5 if right else 7)
             if not ring_end:
-                yield (a_down if right else a_up), pick_flag(zfirst, True if right else below_top, True)
-            yield b_up, pick_flag(zfirst, zz < z, below_top)
-            yield b_down, pick_flag(zfirst, zz < z, z < far_right(k))
+                going = pick_flag(zfirst, True if right else below_top, True)
+                yield (a_down if right else a_up), going, LANDING[0, right, k + 2]
+            yield b_up, pick_flag(zfirst, zz < z, below_top), LANDING[1, False, k]
+            yield b_down, pick_flag(zfirst, zz < z, z < far_right(k)), LANDING[1, True, k]
         elif right:
             if j < far_right(k):
-                yield b_down, None
+                yield b_down, True, LANDING[j + 1, True, k]
         elif j < far_left(k):
-            yield b_up, pick_flag(zfirst, True, below_top)
-
-    def copies(n, right):
-        event = ORDER[n]
-        at, _, seen, _ = piece_of(event, right, zfirst)
-        spot = buf.at[mine + at]
-        base = n * 8 + (4 if right else 0)
-        yield seen, remote(spot, spot, send_sem.at[base], other_sem.at[at], mate)
-        for place, (device, needed) in enumerate(routes(event, right)):
-            yield needed, remote(spot, spot, send_sem.at[base + 1 + place], own_sem.at[at], device)
-
-    def each_side(n, act):
+            yield b_up, pick_flag(zfirst, True, below_top), LANDING[j + 1, False, k]
+
+    def take(n):
+        sides = []
         for right in (False, True):
             found = piece_of(ORDER[n], right, zfirst)
-            if found is None:
-                continue
-
-            @pl.when(found[1])
-            def _():
-                act(n, right, found[0])
-
-    def take(n, right, at):
-        spot = buf.at[mine + at]
-        remote(spot, spot, send_sem.at[0], own_sem.at[at], b_up).wait_recv()
-        for needed, copy in copies(n, right):
-            if needed is None:
-                copy.start()
-            else:
-                pl.when(needed)(copy.start)
-
-    def finish(n, right, at):
-        for needed, copy in copies(n, right):
-            if needed is None:
-                copy.wait_send()
-            else:
-                pl.when(needed)(copy.wait_send)
-
-    def wait_other(at):
-        spot = buf.at[theirs + at]
-        remote(spot, spot, send_sem.at[0], other_sem.at[at], mate).wait_recv()
+            if found is not None:
+                sides.append((right,) + found)
+        count = sum(comes.astype(jnp.int32) for _, _, comes, _, _ in sides)
+        for many in range(1, len(sides) + 1):
+            spots = buf.at[pl.ds(0, many)]
+            pl.when(count == many)(remote(spots, spots, send_sem, own_sem.at[n], b_up).wait_recv)
+        for right, at, comes, seen, _ in sides:
+            spot = buf.at[mine + at]
+            ways = [(mate, seen, other_sem.at[n // BATCH])]
+            ways += [(device, needed, own_sem.at[land]) for device, needed, land in routes(ORDER[n], right)]
+            for device, needed, sem in ways:
+                needed = jnp.logical_and(comes, needed)
+                sent.append(needed.astype(jnp.int32))
+                pl.when(needed)(remote(spot, spot, send_sem, sem, device).start)
+
+    def wait_other(batch, seen):
+        count = sum(flag.astype(jnp.int32) for flag in seen)
+        for many in range(1, len(seen) + 1):
+            spots = buf.at[pl.ds(0, many)]
+            pl.when(count == many)(remote(spots, spots, send_sem, other_sem.at[batch], mate).wait_recv)
 
     factor = math.log2(math.e) / math.sqrt(WIDTH)
 
@@ -228,7 +254,8 @@
             values, p.astype(jnp.bfloat16), (((0,), (0,)), ((), ())), preferred_element_type=jnp.float32
         )
 
-    wait_other(cell)
+    whole = buf.at[theirs + cell]
+    remote(whole, whole, send_sem, other_sem.at[BATCHES], mate).wait_recv()
     key = lax.broadcasted_iota(jnp.int32, (PIECE, ROWS), 0)
     row = lax.broadcasted_iota(jnp.int32, (PIECE, ROWS), 1) % PIECE
     row_at = jnp.where(row < HALF, row, row + HALF) + core * HALF
@@ -270,23 +297,23 @@
             acc[WIDTH : WIDTH + 1] = acc[WIDTH : WIDTH + 1] * shrink + jnp.sum(p, axis=0, keepdims=True)
             acc[:WIDTH] = acc[:WIDTH] * shrink + fresh
 
-    events = len(ORDER)
-    for start in range(0, events + BATCH, BATCH):
+    for start in range(0, EVENTS + BATCH, BATCH):
         pieces = []
-        for n in range(start, start + BATCH):
-            if n < events:
-                each_side(n, take)
-                for right in (False, True):
-                    found = piece_of(ORDER[n], right, zfirst)
-                    if found is not None:
-                        pieces.append((mine + found[0], found[2]))
-        for n in range(start - BATCH, start):
-            if n >= 0:
+        for n in range(start, min(start + BATCH, EVENTS)):
+            take(n)
+            for right in (False, True):
+                found = piece_of(ORDER[n], right, zfirst)
+                if found is not None:
+                    pieces.append((mine + found[0], found[2]))
+        if start > 0:
+            theirs_now = []
+            for n in range(start - BATCH, start):
                 for right in (False, True):
                     found = piece_of(ORDER[n], right, jnp.logical_not(zfirst))
                     if found is not None:
-                        pl.when(found[2])(functools.partial(wait_other, found[0]))
-                        pieces.append((theirs + found[0], found[2]))
+                        theirs_now.append((theirs + found[0], found[2]))
+            wait_other(start // BATCH - 1, [seen for _, seen in theirs_now])
+            pieces += theirs_now
         attend(pieces)
 
     o = (acc[:WIDTH] / acc[WIDTH : WIDTH + 1]).T.astype(jnp.bfloat16)
@@ -294,44 +321,50 @@
     heads = pl.ds(pl.multiple_of(tp * 8 + xh * 4, 4), GROUP)
     places = ((xh, 1 - tp, side), (1 - xh, tp, swap), (1 - xh, 1 - tp, cross))
     for at, (to_xh, to_tp, device) in enumerate(places):
-        remote(obuf.at[:, to_xh, to_tp], out_ref.at[heads], out_send.at[at], out_recv.at[at], device).start()
-    out_ref[heads] = obuf[:, xh, tp]
+        remote(obuf.at[:, to_xh, to_tp], landed.at[heads], out_send.at[at], out_recv.at[at], device).start()
+    landed[heads] = obuf[:, xh, tp]
     kv_out.wait_send()
     q_out.wait_send()
-    whole = buf.at[own]
-    for at, (device, needed) in enumerate(first_targets):
-        pl.when(needed)(remote(whole, whole, first_send.at[at], own_sem.at[cell], device).wait_send)
-    remote(whole, whole, first_send.at[4], other_sem.at[cell], mate).wait_send()
-    for n in range(events):
-        each_side(n, finish)
+    total = sum(sent)
+    for many in TOTALS:
+        spots = buf.at[pl.ds(0, many)]
+        pl.when(total == many)(remote(spots, spots, send_sem, own_sem.at[0], b_up).wait_send)
     for at, (to_xh, to_tp, device) in enumerate(places):
         from_heads = pl.ds(pl.multiple_of(to_tp * 8 + to_xh * 4, 4), GROUP)
-        remote(obuf.at[:, to_xh, to_tp], out_ref.at[from_heads], out_send.at[at], out_recv.at[at], device).wait()
+        remote(obuf.at[:, to_xh, to_tp], landed.at[from_heads], out_send.at[at], out_recv.at[at], device).wait()
+    out_ref[...] = jnp.swapaxes(landed[...].astype(jnp.float32), 0, 1).astype(jnp.bfloat16)
 
 
 def per_device(queries, incoming_lookup_vectors, incoming_content_vectors):
     tok_rows = queries.shape[0]
     my_index = lax.axis_index("ctx")
     natural_pos = my_index * tok_rows + jnp.arange(tok_rows, dtype=jnp.int32)
-    key_cache = rotate(incoming_lookup_vectors, natural_pos)
-    spun = rotate(queries, natural_pos).transpose(1, 0, 2)
-    pair = jnp.concatenate([key_cache, incoming_content_vectors], axis=-1).transpose(1, 0, 2)
+    half_width = WIDTH // 2
+    inverse_freq = rope_base ** (-(jnp.arange(half_width, dtype=jnp.float32) * 2.0 / WIDTH))
+    angles = natural_pos.astype(jnp.float32)[:, None] * inverse_freq[None, :]
+    cosine = jnp.cos(angles)
+    sine = jnp.sin(angles)
     vmem = pl.BlockSpec(memory_space=pltpu.VMEM)
-    out = pl.pallas_call(
+    return pl.pallas_call(
         kernel,
-        out_shape=jax.ShapeDtypeStruct((16, HALF // 2, WIDTH), jnp.bfloat16),
-        in_specs=[vmem, vmem],
-        out_specs=vmem,
+        out_shape=(
+            jax.ShapeDtypeStruct((HALF // 2, 16, WIDTH), jnp.bfloat16),
+            jax.ShapeDtypeStruct((HALF, 2, WIDTH), jnp.bfloat16),
+        ),
+        in_specs=[vmem] * 5,
+        out_specs=(vmem, vmem),
         scratch_shapes=[
+            pltpu.VMEM((8, HALF, WIDTH), jnp.bfloat16),
+            pltpu.VMEM((2, HALF, 2 * WIDTH), jnp.bfloat16),
+            pltpu.VMEM((16, HALF // 2, WIDTH), jnp.bfloat16),
             pltpu.VMEM((2 * CELLS, PIECE, 2 * WIDTH), jnp.bfloat16),
             pltpu.VMEM((GROUP, 2, HALF, WIDTH), jnp.bfloat16),
             pltpu.VMEM((GROUP, 2, 2, HALF // 2, WIDTH), jnp.bfloat16),
             pltpu.VMEM((WIDTH + 8, ROWS), jnp.float32),
             pltpu.VMEM((8, ROWS), jnp.float32),
-            pltpu.SemaphoreType.DMA((5,)),
-            pltpu.SemaphoreType.DMA((SENDS,)),
-            pltpu.SemaphoreType.DMA((CELLS,)),
-            pltpu.SemaphoreType.DMA((CELLS,)),
+            pltpu.SemaphoreType.DMA,
+            pltpu.SemaphoreType.DMA((EVENTS,)),
+            pltpu.SemaphoreType.DMA((BATCHES + 1,)),
             pltpu.SemaphoreType.DMA((2,)),
             pltpu.SemaphoreType.DMA((2,)),
             pltpu.SemaphoreType.DMA((3,)),
@@ -341,8 +374,13 @@
             collective_id=0, has_side_effects=True, vmem_limit_bytes=48 * 1024 * 1024
         ),
         name="cell_attention",
-    )(spun, pair)
-    return (out.transpose(1, 0, 2), key_cache)
+    )(
+        queries,
+        incoming_lookup_vectors,
+        incoming_content_vectors,
+        jnp.concatenate([cosine, cosine], axis=1),
+        jnp.concatenate([-sine, sine], axis=1),
+    )
 
 
 def solution(mesh):

time: 54.4 us -> 49.7 us (0.914)
  Pallas kernels: 49 us -> 46.6 us
  other arithmetic: 1.66 us -> 0.29 us
  local copies, waits for them, and re-layouts: 2.75 us -> 1.96 us
    pallas_call x1, Pallas kernels: 49 us -> 46.6 us  [per_device(): pl.pallas_call(kernel, out_shape=(jax.ShapeDtypeStruct((HALF // 2, 16, WI...]
    convert_element_type x3 -> x1, other arithmetic: 0.93 us -> 0.01 us  [per_device(): angles = natural_pos.astype(jnp.float32)[:, None] * inverse_freq[None, :]]
    unnamed x7 -> x8, local copies, waits for them, and re-layouts: 2.75 us -> 1.96 us
where the time goes in v3:
time: 49.7 us; the launch traced here: 49.6 us
  Pallas kernels  46.6 us (94%)
  local copies, waits for them, and re-layouts  1.96 us (4%)
  between operations  0.69 us (1%)
    pallas_call x1, Pallas kernels, per_device(): pl.pallas_call(kernel, out_shape=(jax.ShapeDtypeStruct((HALF // 2, 16, WI...  46.6 us
    unnamed x8, local copies, waits for them, and re-layouts  1.96 us

profile of v3, /device:TPU:448, one launch (start us, length us, event | category | flops | bytes accessed | tf_op | source)
XLA Modules:
  0.0 49.6 jit_solution(1326629755341345532)
XLA Ops:
  0.7 0.0 copy-start
  0.7 0.2 fusion
  0.9 0.0 copy-start.1
  0.9 0.0 copy-start.2
  0.9 0.1 pad_maximum_fusion
  1.0 0.6 %copy-done = bf16[64,8,128]{2,1,0:T(8,128)(2,1)S(1)} copy-done((bf16[64,8,128]{2,1,0:T(8,128)(2,1)S(1)}, bf16[64,8,128]{2,1,0:T(8,128)(2,1)}, u32[]{:S(2)}) %copy-start) | copy-done | bytes 131096
  1.6 0.1 copy-done.1
  1.6 0.0 copy-done.2
  1.7 46.6 %cell_attention.1 = (bf16[32,16,128]{2,1,0:T(8,128)(2,1)S(1)}, bf16[64,2,128]{2,1,0:T(2,128)(2,1)S(1)}) custom-call(bf16[64,8,128]{2,1,0:T(8,128)(2,1)S(1)} %copy-done, bf16[64,2,128]{2,1,0:T(2,128)(2,1)S(1)} %copy-done.1, bf16[64,2,128]{2,1,0:T(2,128)(2,1)S(1)} %copy-done.2, f32[64,128]{1,0:T(8,128)S(1)} %get-tuple-element.5.cos_ref, ...), custom_call_target="tpu_custom_call" | custom-call | tf_op jit(solution)/shard_map/cell_attention/pallas_call | solution.py:348
  48.3 0.7 %copy.7 = bf16[32,16,128]{2,1,0:T(8,128)(2,1)} copy(bf16[32,16,128]{2,1,0:T(8,128)(2,1)S(1)} %get-tuple-element.9) | data formatting | bytes 262144
  49.0 0.6 %copy.8 = bf16[64,2,128]{2,1,0:T(2,128)(2,1)} copy(bf16[64,2,128]{2,1,0:T(2,128)(2,1)S(1)} %get-tuple-element.10) | data formatting | bytes 65536
  (2 shorter events, 0.0 us)
Async XLA Ops:
  0.7 0.9 %copy-start = (bf16[64,8,128]{2,1,0:T(8,128)(2,1)S(1)}, bf16[64,8,128]{2,1,0:T(8,128)(2,1)}, u32[]{:S(2)}) copy-start(bf16[64,8,128]{2,1,0:T(8,128)(2,1)} %q_raw.1) | copy-start | bytes 393220
  0.9 0.8 %copy-start.1 = (bf16[64,2,128]{2,1,0:T(2,128)(2,1)S(1)}, bf16[64,2,128]{2,1,0:T(2,128)(2,1)}, u32[]{:S(2)}) copy-start(bf16[64,2,128]{2,1,0:T(2,128)(2,1)} %k_raw.1) | copy-start | bytes 98308
  0.9 0.8 %copy-start.2 = (bf16[64,2,128]{2,1,0:T(2,128)(2,1)S(1)}, bf16[64,2,128]{2,1,0:T(2,128)(2,1)}, u32[]{:S(2)}) copy-start(bf16[64,2,128]{2,1,0:T(2,128)(2,1)} %v_raw.1) | copy-start | bytes 98308

commit v4 on v3

--- a/solution.py
+++ b/solution.py
@@ -32,20 +32,27 @@
     return 7 - far_left(k)
 
 
-def event_order():
-    entries = [(i, 0, 2 * i - 1, 2 * i if i < 4 else None) for i in range(1, 5)]
-    for j in range(1, 4):
-        for k in range(8):
-            entries.append((j + abs(offset_of(k)), j, k, k))
-    for left, right in ((0, 1), (3, 2), (4, 5), (7, 6)):
-        entries.append((4 + max(abs(offset_of(left)), abs(offset_of(right))), 4, left, right))
-    entries.sort(key=lambda e: e[:3])
-    return [e[1:] for e in entries]
-
-
-ORDER = event_order()
+ORDER = (
+    (0, 1, 2), (1, 0, 0), (0, 3, 4), (1, 1, 1), (1, 2, 2), (0, 5, 6), (2, 1, 1), (1, 4, 4),
+    (0, 7, None), (1, 3, 3), (1, 5, 5), (1, 6, 6), (2, 4, 4), (2, 2, 2), (1, 7, 7), (2, 3, 3),
+    (2, 0, 0), (2, 6, 6), (2, 5, 5), (3, 2, 2), (2, 7, 7), (3, 1, 1), (3, 0, 0), (3, 3, 3),
+    (3, 6, 6), (3, 4, 4), (3, 5, 5), (3, 7, 7), (4, 3, 2), (4, 0, 1), (4, 4, 5), (4, 7, 6),
+)
 EVENTS = len(ORDER)
-BATCHES = EVENTS // BATCH
+
+
+def schedule():
+    groups = [(n, n + 1) for n in range(0, EVENTS - 2, BATCH)] + [(EVENTS - 2,), (EVENTS - 1,)]
+    steps = [(groups[0], ())]
+    for at in range(1, len(groups) - 1):
+        steps.append((groups[at], (at - 1,)))
+    last = len(groups) - 1
+    steps.append((groups[last], (last - 1, last)))
+    return groups, steps
+
+
+GROUPS, STEPS = schedule()
+GROUP_OF = {n: at for at, group in enumerate(GROUPS) for n in group}
 
 
 def landing_events():
@@ -165,25 +172,23 @@
         (b_down, pick_flag(zfirst, True, low)),
     )
 
+    halves = (keep_rows, get_rows)
     first_sems = (LANDING[0, False, 1], LANDING[0, True, 2], LANDING[1, False, 0], LANDING[1, True, 0])
     sent = [jnp.int32(1)] + [needed.astype(jnp.int32) for _, needed in first_targets]
 
-    def start_first(src, part):
+    def start_first(src, half):
+        part = halves[half]
         for at, (device, needed) in zip(first_sems, first_targets):
-            pl.when(needed)(remote(src, buf.at[own, part], send_sem, own_sem.at[at], device).start)
-        remote(src, buf.at[own, part], send_sem, other_sem.at[BATCHES], mate).start()
-
-    start_first(kv_ref.at[xh], keep_rows)
+            pl.when(needed)(remote(src, buf.at[own, part], send_sem, own_sem.at[half, at], device).start)
+        remote(src, buf.at[own, part], send_sem, other_sem.at[len(GROUPS)], mate).start()
+
+    start_first(kv_ref.at[xh], 0)
     other_heads = pl.ds(pl.multiple_of((1 - xh) * GROUP, GROUP), GROUP)
     own_heads = pl.ds(pl.multiple_of(xh * GROUP, GROUP), GROUP)
     q_out = remote(q_ref.at[other_heads], qbuf.at[:, xh], swap_send.at[1], swap_recv.at[1], swap)
     q_out.start()
     buf[own, keep_rows] = kv_ref[xh]
     qbuf[:, xh] = q_ref[own_heads]
-
-    remote(kv_ref.at[1 - xh], buf.at[own, get_rows], swap_send.at[0], swap_recv.at[0], swap).wait_recv()
-    start_first(buf.at[own, get_rows], get_rows)
-    remote(q_ref.at[other_heads], qbuf.at[:, 1 - xh], swap_send.at[1], swap_recv.at[1], swap).wait_recv()
 
     def piece_of(event, right, first_z):
         j, kl, kr = event
@@ -218,7 +223,7 @@
         elif j < far_left(k):
             yield b_up, pick_flag(zfirst, True, below_top), LANDING[j + 1, False, k]
 
-    def take(n):
+    def take(n, half):
         sides = []
         for right in (False, True):
             found = piece_of(ORDER[n], right, zfirst)
@@ -226,16 +231,20 @@
                 sides.append((right,) + found)
         count = sum(comes.astype(jnp.int32) for _, _, comes, _, _ in sides)
         for many in range(1, len(sides) + 1):
-            spots = buf.at[pl.ds(0, many)]
-            pl.when(count == many)(remote(spots, spots, send_sem, own_sem.at[n], b_up).wait_recv)
+            spots = buf.at[pl.ds(0, many), pl.ds(0, HALF)]
+            pl.when(count == many)(remote(spots, spots, send_sem, own_sem.at[half, n], b_up).wait_recv)
         for right, at, comes, seen, _ in sides:
-            spot = buf.at[mine + at]
-            ways = [(mate, seen, other_sem.at[n // BATCH])]
-            ways += [(device, needed, own_sem.at[land]) for device, needed, land in routes(ORDER[n], right)]
-            for device, needed, sem in ways:
+            spot = buf.at[mine + at, halves[half]]
+            for device, needed, land in routes(ORDER[n], right):
                 needed = jnp.logical_and(comes, needed)
+                pl.when(needed)(remote(spot, spot, send_sem, own_sem.at[half, land], device).start)
+                if half:
+                    sent.append(needed.astype(jnp.int32))
+            if half:
+                needed = jnp.logical_and(comes, seen)
+                whole = buf.at[mine + at]
+                pl.when(needed)(remote(whole, whole, send_sem, other_sem.at[GROUP_OF[n]], mate).start)
                 sent.append(needed.astype(jnp.int32))
-                pl.when(needed)(remote(spot, spot, send_sem, sem, device).start)
 
     def wait_other(batch, seen):
         count = sum(flag.astype(jnp.int32) for flag in seen)
@@ -243,6 +252,13 @@
             spots = buf.at[pl.ds(0, many)]
             pl.when(count == many)(remote(spots, spots, send_sem, other_sem.at[batch], mate).wait_recv)
 
+    for n in GROUPS[0]:
+        take(n, 0)
+
+    remote(kv_ref.at[1 - xh], buf.at[own, get_rows], swap_send.at[0], swap_recv.at[0], swap).wait_recv()
+    start_first(buf.at[own, get_rows], 1)
+    remote(q_ref.at[other_heads], qbuf.at[:, 1 - xh], swap_send.at[1], swap_recv.at[1], swap).wait_recv()
+
     factor = math.log2(math.e) / math.sqrt(WIDTH)
 
     def scores_of(keys):
@@ -255,7 +271,7 @@
         )
 
     whole = buf.at[theirs + cell]
-    remote(whole, whole, send_sem, other_sem.at[BATCHES], mate).wait_recv()
+    remote(whole, whole, send_sem, other_sem.at[len(GROUPS)], mate).wait_recv()
     key = lax.broadcasted_iota(jnp.int32, (PIECE, ROWS), 0)
     row = lax.broadcasted_iota(jnp.int32, (PIECE, ROWS), 1) % PIECE
     row_at = jnp.where(row < HALF, row, row + HALF) + core * HALF
@@ -297,22 +313,25 @@
             acc[WIDTH : WIDTH + 1] = acc[WIDTH : WIDTH + 1] * shrink + jnp.sum(p, axis=0, keepdims=True)
             acc[:WIDTH] = acc[:WIDTH] * shrink + fresh
 
-    for start in range(0, EVENTS + BATCH, BATCH):
+    for fresh_events, shared in STEPS:
         pieces = []
-        for n in range(start, min(start + BATCH, EVENTS)):
-            take(n)
+        for half in (0, 1):
+            for n in fresh_events:
+                if half or n not in GROUPS[0]:
+                    take(n, half)
+        for n in fresh_events:
             for right in (False, True):
                 found = piece_of(ORDER[n], right, zfirst)
                 if found is not None:
                     pieces.append((mine + found[0], found[2]))
-        if start > 0:
+        for group in shared:
             theirs_now = []
-            for n in range(start - BATCH, start):
+            for n in GROUPS[group]:
                 for right in (False, True):
                     found = piece_of(ORDER[n], right, jnp.logical_not(zfirst))
                     if found is not None:
                         theirs_now.append((theirs + found[0], found[2]))
-            wait_other(start // BATCH - 1, [seen for _, seen in theirs_now])
+            wait_other(group, [seen for _, seen in theirs_now])
             pieces += theirs_now
         attend(pieces)
 
@@ -328,7 +347,7 @@
     total = sum(sent)
     for many in TOTALS:
         spots = buf.at[pl.ds(0, many)]
-        pl.when(total == many)(remote(spots, spots, send_sem, own_sem.at[0], b_up).wait_send)
+        pl.when(total == many)(remote(spots, spots, send_sem, own_sem.at[0, 0], b_up).wait_send)
     for at, (to_xh, to_tp, device) in enumerate(places):
         from_heads = pl.ds(pl.multiple_of(to_tp * 8 + to_xh * 4, 4), GROUP)
         remote(obuf.at[:, to_xh, to_tp], landed.at[from_heads], out_send.at[at], out_recv.at[at], device).wait()
@@ -363,8 +382,8 @@
             pltpu.VMEM((WIDTH + 8, ROWS), jnp.float32),
             pltpu.VMEM((8, ROWS), jnp.float32),
             pltpu.SemaphoreType.DMA,
-            pltpu.SemaphoreType.DMA((EVENTS,)),
-            pltpu.SemaphoreType.DMA((BATCHES + 1,)),
+            pltpu.SemaphoreType.DMA((2, EVENTS)),
+            pltpu.SemaphoreType.DMA((len(GROUPS) + 1,)),
             pltpu.SemaphoreType.DMA((2,)),
             pltpu.SemaphoreType.DMA((2,)),
             pltpu.SemaphoreType.DMA((3,)),

time: 49.7 us -> 48.3 us (0.972); the launches traced: 49.6 us -> 47.6 us
  Pallas kernels: 46.6 us -> 44.7 us
    pallas_call x1, Pallas kernels: 46.6 us -> 44.7 us  [per_device(): pl.pallas_call(kernel, out_shape=(jax.ShapeDtypeStruct((HALF // 2, 16, WI...]
where the time goes in v4:
time: 48.3 us; the launch traced here: 47.6 us
  Pallas kernels  44.7 us (93%)
  local copies, waits for them, and re-layouts  1.96 us (4%)
  between operations  0.69 us (1%)
    pallas_call x1, Pallas kernels, per_device(): pl.pallas_call(kernel, out_shape=(jax.ShapeDtypeStruct((HALF // 2, 16, WI...  44.7 us
    unnamed x8, local copies, waits for them, and re-layouts  1.96 us

profile of v4, /device:TPU:448, one launch (start us, length us, event | category | flops | bytes accessed | tf_op | source)
XLA Modules:
  0.0 47.6 jit_solution(7132147549357835625)
XLA Ops:
  0.7 0.0 copy-start
  0.7 0.2 fusion
  0.9 0.0 copy-start.1
  0.9 0.0 copy-start.2
  0.9 0.1 pad_maximum_fusion
  1.0 0.6 %copy-done = bf16[64,8,128]{2,1,0:T(8,128)(2,1)S(1)} copy-done((bf16[64,8,128]{2,1,0:T(8,128)(2,1)S(1)}, bf16[64,8,128]{2,1,0:T(8,128)(2,1)}, u32[]{:S(2)}) %copy-start) | copy-done | bytes 131096
  1.6 0.1 copy-done.1
  1.6 0.0 copy-done.2
  1.7 44.7 %cell_attention.1 = (bf16[32,16,128]{2,1,0:T(8,128)(2,1)S(1)}, bf16[64,2,128]{2,1,0:T(2,128)(2,1)S(1)}) custom-call(bf16[64,8,128]{2,1,0:T(8,128)(2,1)S(1)} %copy-done, bf16[64,2,128]{2,1,0:T(2,128)(2,1)S(1)} %copy-done.1, bf16[64,2,128]{2,1,0:T(2,128)(2,1)S(1)} %copy-done.2, f32[64,128]{1,0:T(8,128)S(1)} %get-tuple-element.5.cos_ref, ...), custom_call_target="tpu_custom_call" | custom-call | tf_op jit(solution)/shard_map/cell_attention/pallas_call | solution.py:367
  46.4 0.7 %copy.7 = bf16[32,16,128]{2,1,0:T(8,128)(2,1)} copy(bf16[32,16,128]{2,1,0:T(8,128)(2,1)S(1)} %get-tuple-element.9) | data formatting | bytes 262144
  47.0 0.6 %copy.8 = bf16[64,2,128]{2,1,0:T(2,128)(2,1)} copy(bf16[64,2,128]{2,1,0:T(2,128)(2,1)S(1)} %get-tuple-element.10) | data formatting | bytes 65536
  (2 shorter events, 0.0 us)
Async XLA Ops:
  0.7 0.9 %copy-start = (bf16[64,8,128]{2,1,0:T(8,128)(2,1)S(1)}, bf16[64,8,128]{2,1,0:T(8,128)(2,1)}, u32[]{:S(2)}) copy-start(bf16[64,8,128]{2,1,0:T(8,128)(2,1)} %q_raw.1) | copy-start | bytes 393220
  0.9 0.8 %copy-start.1 = (bf16[64,2,128]{2,1,0:T(2,128)(2,1)S(1)}, bf16[64,2,128]{2,1,0:T(2,128)(2,1)}, u32[]{:S(2)}) copy-start(bf16[64,2,128]{2,1,0:T(2,128)(2,1)} %k_raw.1) | copy-start | bytes 98308
  0.9 0.8 %copy-start.2 = (bf16[64,2,128]{2,1,0:T(2,128)(2,1)S(1)}, bf16[64,2,128]{2,1,0:T(2,128)(2,1)}, u32[]{:S(2)}) copy-start(bf16[64,2,128]{2,1,0:T(2,128)(2,1)} %v_raw.1) | copy-start | bytes 98308

commit v5 on v4

--- a/solution.py
+++ b/solution.py
@@ -47,7 +47,8 @@
     for at in range(1, len(groups) - 1):
         steps.append((groups[at], (at - 1,)))
     last = len(groups) - 1
-    steps.append((groups[last], (last - 1, last)))
+    steps.append((groups[last], (last - 1,)))
+    steps.append(((), (last,)))
     return groups, steps
 
 
@@ -99,7 +100,7 @@
 TOTALS = sorted({sends_of(f, z, y) for f in (True, False) for z in range(RING) for y in range(RING)})
 
 
-def kernel(q_raw, k_raw, v_raw, cos_ref, sin_ref, out_ref, key_ref, q_ref, kv_ref, landed, buf, qbuf, obuf, acc, top, send_sem, own_sem, other_sem, swap_send, swap_recv, out_send, out_recv):
+def kernel(q_raw, k_raw, v_raw, cos_ref, sin_ref, landed, key_ref, q_ref, kv_ref, buf, qbuf, obuf, acc, top, send_sem, own_sem, other_sem, swap_send, swap_recv, out_send, out_recv):
     ctx = lax.axis_index("ctx")
     tp = lax.axis_index("tp")
     core = ctx % 2
@@ -351,7 +352,11 @@
     for at, (to_xh, to_tp, device) in enumerate(places):
         from_heads = pl.ds(pl.multiple_of(to_tp * 8 + to_xh * 4, 4), GROUP)
         remote(obuf.at[:, to_xh, to_tp], landed.at[from_heads], out_send.at[at], out_recv.at[at], device).wait()
-    out_ref[...] = jnp.swapaxes(landed[...].astype(jnp.float32), 0, 1).astype(jnp.bfloat16)
+
+
+def finish(by_head, keys, out_ref, key_ref):
+    key_ref[...] = keys[...]
+    out_ref[...] = jnp.swapaxes(by_head[...].astype(jnp.float32), 0, 1).astype(jnp.bfloat16)
 
 
 def per_device(queries, incoming_lookup_vectors, incoming_content_vectors):
@@ -364,10 +369,10 @@
     cosine = jnp.cos(angles)
     sine = jnp.sin(angles)
     vmem = pl.BlockSpec(memory_space=pltpu.VMEM)
-    return pl.pallas_call(
+    by_head, keys = pl.pallas_call(
         kernel,
         out_shape=(
-            jax.ShapeDtypeStruct((HALF // 2, 16, WIDTH), jnp.bfloat16),
+            jax.ShapeDtypeStruct((16, HALF // 2, WIDTH), jnp.bfloat16),
             jax.ShapeDtypeStruct((HALF, 2, WIDTH), jnp.bfloat16),
         ),
         in_specs=[vmem] * 5,
@@ -375,7 +380,6 @@
         scratch_shapes=[
             pltpu.VMEM((8, HALF, WIDTH), jnp.bfloat16),
             pltpu.VMEM((2, HALF, 2 * WIDTH), jnp.bfloat16),
-            pltpu.VMEM((16, HALF // 2, WIDTH), jnp.bfloat16),
             pltpu.VMEM((2 * CELLS, PIECE, 2 * WIDTH), jnp.bfloat16),
             pltpu.VMEM((GROUP, 2, HALF, WIDTH), jnp.bfloat16),
             pltpu.VMEM((GROUP, 2, 2, HALF // 2, WIDTH), jnp.bfloat16),
@@ -400,6 +404,17 @@
         jnp.concatenate([cosine, cosine], axis=1),
         jnp.concatenate([-sine, sine], axis=1),
     )
+    return pl.pallas_call(
+        finish,
+        out_shape=(
+            jax.ShapeDtypeStruct((HALF // 2, 16, WIDTH), jnp.bfloat16),
+            jax.ShapeDtypeStruct((HALF, 2, WIDTH), jnp.bfloat16),
+        ),
+        in_specs=[vmem] * 2,
+        out_specs=(vmem, vmem),
+        compiler_params=pltpu.CompilerParams(vmem_limit_bytes=8 * 1024 * 1024),
+        name="token_order",
+    )(by_head, keys)
 
 
 def solution(mesh):

time: 48.3 us -> 47.4 us (0.981)
  local copies, waits for them, and re-layouts: 1.96 us -> 0.69 us
    unnamed x8 -> x6, local copies, waits for them, and re-layouts: 1.96 us -> 0.69 us
    pallas_call x1 -> x2, Pallas kernels: 44.7 us -> 45 us  [the longest x1 44.3 us: per_device(): pl.pallas_call(kernel, out_shape=(jax.ShapeDtypeStruct((16, HALF // 2, WI...]
where the time goes in v5:
time: 47.4 us; the launch traced here: 46.7 us
  Pallas kernels  45 us (95%)
  local copies, waits for them, and re-layouts  0.69 us (1%)
  between operations  0.69 us (1%)
    pallas_call x1, Pallas kernels, per_device(): pl.pallas_call(kernel, out_shape=(jax.ShapeDtypeStruct((16, HALF // 2, WI...  44.3 us

profile of v5, /device:TPU:448, one launch (start us, length us, event | category | flops | bytes accessed | tf_op | source)
XLA Modules:
  0.0 46.7 jit_solution(16324930429650216662)
XLA Ops:
  0.7 0.0 copy-start
  0.7 0.2 fusion
  0.9 0.0 copy-start.1
  0.9 0.0 copy-start.2
  0.9 0.1 pad_maximum_fusion
  1.0 0.6 %copy-done = bf16[64,8,128]{2,1,0:T(8,128)(2,1)S(1)} copy-done((bf16[64,8,128]{2,1,0:T(8,128)(2,1)S(1)}, bf16[64,8,128]{2,1,0:T(8,128)(2,1)}, u32[]{:S(2)}) %copy-start) | copy-done | bytes 131096
  1.6 0.1 copy-done.1
  1.6 0.0 copy-done.2
  1.7 44.3 %cell_attention.1 = (bf16[16,32,128]{2,1,0:T(8,128)(2,1)S(1)}, bf16[64,2,128]{2,1,0:T(2,128)(2,1)S(1)}) custom-call(bf16[64,8,128]{2,1,0:T(8,128)(2,1)S(1)} %copy-done, bf16[64,2,128]{2,1,0:T(2,128)(2,1)S(1)} %copy-done.1, bf16[64,2,128]{2,1,0:T(2,128)(2,1)S(1)} %copy-done.2, f32[64,128]{1,0:T(8,128)S(1)} %get-tuple-element.9.cos_ref, ...), custom_call_target="tpu_custom_call" | custom-call | tf_op jit(solution)/shard_map/cell_attention/pallas_call | solution.py:372
  45.9 0.7 %token_order.1 = (bf16[32,16,128]{2,1,0:T(8,128)(2,1)}, bf16[64,2,128]{2,1,0:T(2,128)(2,1)}) custom-call(bf16[16,32,128]{2,1,0:T(8,128)(2,1)S(1)} %get-tuple-element.4.by_head, bf16[64,2,128]{2,1,0:T(2,128)(2,1)S(1)} %get-tuple-element.5.keys), custom_call_target="tpu_custom_call" | custom-call | tf_op jit(solution)/shard_map/token_order/pallas_call | solution.py:407
  (2 shorter events, 0.0 us)
Async XLA Ops:
  0.7 0.9 %copy-start = (bf16[64,8,128]{2,1,0:T(8,128)(2,1)S(1)}, bf16[64,8,128]{2,1,0:T(8,128)(2,1)}, u32[]{:S(2)}) copy-start(bf16[64,8,128]{2,1,0:T(8,128)(2,1)} %q_raw.1) | copy-start | bytes 393220
  0.9 0.8 %copy-start.1 = (bf16[64,2,128]{2,1,0:T(2,128)(2,1)S(1)}, bf16[64,2,128]{2,1,0:T(2,128)(2,1)}, u32[]{:S(2)}) copy-start(bf16[64,2,128]{2,1,0:T(2,128)(2,1)} %k_raw.1) | copy-start | bytes 98308
  0.9 0.8 %copy-start.2 = (bf16[64,2,128]{2,1,0:T(2,128)(2,1)S(1)}, bf16[64,2,128]{2,1,0:T(2,128)(2,1)}, u32[]{:S(2)}) copy-start(bf16[64,2,128]{2,1,0:T(2,128)(2,1)} %v_raw.1) | copy-start | bytes 98308

commit v6 on v5

--- a/solution.py
+++ b/solution.py
@@ -18,6 +18,8 @@
 GROUP = 4
 ROWS = GROUP * PIECE
 BATCH = 2
+FEW = 4
+WHOLE = 16
 
 
 def offset_of(k):
@@ -225,6 +227,8 @@
             yield b_up, pick_flag(zfirst, True, below_top), LANDING[j + 1, False, k]
 
     def take(n, half):
+        if n >= WHOLE and not half:
+            return
         sides = []
         for right in (False, True):
             found = piece_of(ORDER[n], right, zfirst)
@@ -232,11 +236,13 @@
                 sides.append((right,) + found)
         count = sum(comes.astype(jnp.int32) for _, _, comes, _, _ in sides)
         for many in range(1, len(sides) + 1):
-            spots = buf.at[pl.ds(0, many), pl.ds(0, HALF)]
+            spots = buf.at[pl.ds(0, many), pl.ds(0, PIECE if n >= WHOLE else HALF)]
             pl.when(count == many)(remote(spots, spots, send_sem, own_sem.at[half, n], b_up).wait_recv)
         for right, at, comes, seen, _ in sides:
-            spot = buf.at[mine + at, halves[half]]
             for device, needed, land in routes(ORDER[n], right):
+                if land >= WHOLE and not half:
+                    continue
+                spot = buf.at[mine + at] if land >= WHOLE else buf.at[mine + at, halves[half]]
                 needed = jnp.logical_and(comes, needed)
                 pl.when(needed)(remote(spot, spot, send_sem, own_sem.at[half, land], device).start)
                 if half:
@@ -293,26 +299,38 @@
     acc[:WIDTH] = weigh(jnp.concatenate([buf[piece, :, WIDTH:] for piece in both], axis=0), p)
 
     def attend(pieces):
-        some = pieces[0][1]
-        for _, seen in pieces[1:]:
-            some = jnp.logical_or(some, seen)
-
-        @pl.when(some)
-        def _():
-            spots = [jnp.where(seen, piece, own) for piece, seen in pieces]
-            hide = [jnp.where(seen, 0.0, 1e30) for _, seen in pieces]
-            s = scores_of(jnp.concatenate([buf[at, :, :WIDTH] for at in spots], axis=0))
-            parts = [s[at * PIECE : (at + 1) * PIECE] for at in range(len(pieces))]
-            old = top[0:1]
-            new = old
-            for part, away in zip(parts, hide):
-                new = jnp.maximum(new, jnp.max(part, axis=0, keepdims=True) - away)
-            top[0:1] = new
-            shrink = jnp.exp2((old - new) * factor)
-            p = jnp.concatenate([jnp.exp2((part - (new + away)) * factor) for part, away in zip(parts, hide)], axis=0)
-            fresh = weigh(jnp.concatenate([buf[at, :, WIDTH:] for at in spots], axis=0), p)
-            acc[WIDTH : WIDTH + 1] = acc[WIDTH : WIDTH + 1] * shrink + jnp.sum(p, axis=0, keepdims=True)
-            acc[:WIDTH] = acc[:WIDTH] * shrink + fresh
+        count = jnp.int32(0)
+        ranks = []
+        for _, seen in pieces:
+            ranks.append(count)
+            count = count + seen.astype(jnp.int32)
+        if len(pieces) <= FEW:
+            pl.when(count > 0)(functools.partial(attend_to, pieces))
+            return
+        few = []
+        for place in range(FEW):
+            at = jnp.int32(0)
+            for (piece, seen), rank in zip(pieces, ranks):
+                at = at + jnp.where(jnp.logical_and(seen, rank == place), piece, 0)
+            few.append((at, place < count))
+        pl.when(jnp.logical_and(count > 0, count <= FEW))(functools.partial(attend_to, few))
+        pl.when(count > FEW)(functools.partial(attend_to, pieces))
+
+    def attend_to(pieces):
+        spots = [jnp.where(seen, piece, own) for piece, seen in pieces]
+        hide = [jnp.where(seen, 0.0, 1e30) for _, seen in pieces]
+        s = scores_of(jnp.concatenate([buf[at, :, :WIDTH] for at in spots], axis=0))
+        parts = [s[at * PIECE : (at + 1) * PIECE] for at in range(len(pieces))]
+        old = top[0:1]
+        new = old
+        for part, away in zip(parts, hide):
+            new = jnp.maximum(new, jnp.max(part, axis=0, keepdims=True) - away)
+        top[0:1] = new
+        shrink = jnp.exp2((old - new) * factor)
+        p = jnp.concatenate([jnp.exp2((part - (new + away)) * factor) for part, away in zip(parts, hide)], axis=0)
+        fresh = weigh(jnp.concatenate([buf[at, :, WIDTH:] for at in spots], axis=0), p)
+        acc[WIDTH : WIDTH + 1] = acc[WIDTH : WIDTH + 1] * shrink + jnp.sum(p, axis=0, keepdims=True)
+        acc[:WIDTH] = acc[:WIDTH] * shrink + fresh
 
     for fresh_events, shared in STEPS:
         pieces = []

time: 47.4 us -> 47.2 us (level); the launches traced: 46.7 us -> 47 us
  no operation moved by 1% of the time
where the time goes in v6:
time: 47.2 us; the launch traced here: 47 us
  Pallas kernels  45.4 us (96%)
  local copies, waits for them, and re-layouts  0.69 us (1%)
  between operations  0.69 us (1%)
    pallas_call x1, Pallas kernels, per_device(): pl.pallas_call(kernel, out_shape=(jax.ShapeDtypeStruct((16, HALF // 2, WI...  44.6 us

profile of v6, /device:TPU:448, one launch (start us, length us, event | category | flops | bytes accessed | tf_op | source)
XLA Modules:
  0.0 47.0 jit_solution(3922900292253140135)
XLA Ops:
  0.7 0.0 copy-start
  0.7 0.2 fusion
  0.9 0.0 copy-start.1
  0.9 0.0 copy-start.2
  0.9 0.1 pad_maximum_fusion
  1.0 0.6 %copy-done = bf16[64,8,128]{2,1,0:T(8,128)(2,1)S(1)} copy-done((bf16[64,8,128]{2,1,0:T(8,128)(2,1)S(1)}, bf16[64,8,128]{2,1,0:T(8,128)(2,1)}, u32[]{:S(2)}) %copy-start) | copy-done | bytes 131096
  1.6 0.1 copy-done.1
  1.6 0.0 copy-done.2
  1.7 44.6 %cell_attention.1 = (bf16[16,32,128]{2,1,0:T(8,128)(2,1)S(1)}, bf16[64,2,128]{2,1,0:T(2,128)(2,1)S(1)}) custom-call(bf16[64,8,128]{2,1,0:T(8,128)(2,1)S(1)} %copy-done, bf16[64,2,128]{2,1,0:T(2,128)(2,1)S(1)} %copy-done.1, bf16[64,2,128]{2,1,0:T(2,128)(2,1)S(1)} %copy-done.2, f32[64,128]{1,0:T(8,128)S(1)} %get-tuple-element.9.cos_ref, ...), custom_call_target="tpu_custom_call" | custom-call | tf_op jit(solution)/shard_map/cell_attention/pallas_call | solution.py:390
  46.3 0.7 %token_order.1 = (bf16[32,16,128]{2,1,0:T(8,128)(2,1)}, bf16[64,2,128]{2,1,0:T(2,128)(2,1)}) custom-call(bf16[16,32,128]{2,1,0:T(8,128)(2,1)S(1)} %get-tuple-element.4.by_head, bf16[64,2,128]{2,1,0:T(2,128)(2,1)S(1)} %get-tuple-element.5.keys), custom_call_target="tpu_custom_call" | custom-call | tf_op jit(solution)/shard_map/token_order/pallas_call | solution.py:425
  (2 shorter events, 0.0 us)
Async XLA Ops:
  0.7 0.9 %copy-start = (bf16[64,8,128]{2,1,0:T(8,128)(2,1)S(1)}, bf16[64,8,128]{2,1,0:T(8,128)(2,1)}, u32[]{:S(2)}) copy-start(bf16[64,8,128]{2,1,0:T(8,128)(2,1)} %q_raw.1) | copy-start | bytes 393220
  0.9 0.8 %copy-start.1 = (bf16[64,2,128]{2,1,0:T(2,128)(2,1)S(1)}, bf16[64,2,128]{2,1,0:T(2,128)(2,1)}, u32[]{:S(2)}) copy-start(bf16[64,2,128]{2,1,0:T(2,128)(2,1)} %k_raw.1) | copy-start | bytes 98308
  0.9 0.8 %copy-start.2 = (bf16[64,2,128]{2,1,0:T(2,128)(2,1)S(1)}, bf16[64,2,128]{2,1,0:T(2,128)(2,1)}, u32[]{:S(2)}) copy-start(bf16[64,2,128]{2,1,0:T(2,128)(2,1)} %v_raw.1) | copy-start | bytes 98308
